TPU v7x, 32 devices: a 4x2x2 block of a 4x4x8 slice. The times are simulated.
32 devices in a mesh: dp: 4 (over y, z), fsdp: 8 (over x, core).
Axes of the slice: x: 4, y: 2, z: 2, core: 2. Of those that a mesh axis runs over, the one named last changes fastest.
The devices are a block of a 4x4x8 slice.
Arguments:
- tokens: bfloat16 [512, 128, 2560], P(('dp', 'fsdp')), parts along dimension 0
- gain_in: bfloat16 [2560], P('fsdp')
- w_dq: bfloat16 [2560, 768], P('fsdp')
- gain_q: bfloat16 [768], P('fsdp')
- w_uq: bfloat16 [768, 3840], P('fsdp')
- w_dkv: bfloat16 [2560, 288], P('fsdp')
- gain_kv: bfloat16 [256], P('fsdp')
- w_ukv: bfloat16 [256, 5120], P('fsdp')
- w_out: bfloat16 [2560, 2560], P('fsdp')
Outputs:
- output 1: bfloat16 [512, 128, 2560], P(('dp', 'fsdp')), parts along dimension 0
- output 2: bfloat16 [512, 128, 256], P(('dp', 'fsdp')), parts along dimension 0
- output 3: bfloat16 [512, 128, 32], P(('dp', 'fsdp')), parts along dimension 0
There are 4 independent parts. A program takes and returns all parts, laid end to end along the dimension named above; an argument that names none is the same for every part.
All inputs are finite; a program needn't handle non-finite values.
Results may differ from a plain program's by a relative error of at most 0.00648171.
Values are sent between devices in bfloat16 or wider.
A program may use at most 768 MiB of HBM per device.

v0:
```python
import jax
import jax.numpy as jnp
from jax import lax
from jax.sharding import PartitionSpec as P, NamedSharding

EPSILON = 1e-6
ROPE_THETA = 10000.0


def rms_scale(values_in, gain_vec):
    values_f32 = values_in.astype(jnp.float32)
    inv_rms = lax.rsqrt(jnp.mean(values_f32 * values_f32, axis=-1, keepdims=True) + EPSILON)
    return values_f32 * inv_rms * gain_vec.astype(jnp.float32)


def rope_tables(seq_len, rope_dim):
    half_dim = rope_dim // 2
    inv_freq = ROPE_THETA ** (-2.0 * jnp.arange(half_dim, dtype=jnp.float32) / rope_dim)
    angles = jnp.arange(seq_len, dtype=jnp.float32)[:, None] * inv_freq[None, :]
    return jnp.cos(angles), jnp.sin(angles)


def apply_rope(values_in, cos_t, sin_t):
    half_dim = values_in.shape[-1] // 2
    lo_half = values_in[..., :half_dim]
    hi_half = values_in[..., half_dim:]
    return jnp.concatenate([lo_half * cos_t - hi_half * sin_t, hi_half * cos_t + lo_half * sin_t], axis=-1)


def head_dims(w_uq, w_dkv, gain_kv, w_ukv, w_out):
    rope_dim = w_dkv.shape[1] - gain_kv.shape[0]
    nope_total = w_ukv.shape[1] - w_out.shape[0]
    n_heads = (w_uq.shape[1] - nope_total) // rope_dim
    return n_heads, nope_total // n_heads, rope_dim, w_out.shape[0] // n_heads


def latents(tokens, gain_in, w_dq, gain_q, w_dkv, gain_kv, cos_t, sin_t):
    kv_rank = gain_kv.shape[0]
    normed = rms_scale(tokens, gain_in).astype(jnp.bfloat16)
    q_down = jnp.einsum('btd,dr->btr', normed, w_dq, preferred_element_type=jnp.float32)
    q_lat = rms_scale(q_down, gain_q).astype(jnp.bfloat16)
    kv_down = jnp.einsum('btd,dr->btr', normed, w_dkv, preferred_element_type=jnp.float32)
    latent = rms_scale(kv_down[:, :, :kv_rank], gain_kv).astype(jnp.bfloat16)
    k_pe = apply_rope(kv_down[:, :, kv_rank:], cos_t, sin_t).astype(jnp.bfloat16)
    return q_lat, latent, k_pe


def attend(q_lat, latent, k_pe, w_uq, w_ukv, w_out, head_info, cos_t, sin_t):
    n_heads, nope_dim, rope_dim, v_dim = head_info
    n_prompts = q_lat.shape[0]
    seq_len = q_lat.shape[1]
    q_full = jnp.einsum('btr,rc->btc', q_lat, w_uq, preferred_element_type=jnp.float32)
    q_full = q_full.reshape(n_prompts, seq_len, n_heads, nope_dim + rope_dim)
    q_nope = q_full[..., :nope_dim].astype(jnp.bfloat16)
    q_pe = apply_rope(q_full[..., nope_dim:], cos_t[:, None, :], sin_t[:, None, :]).astype(jnp.bfloat16)
    kv_up = jnp.einsum('btr,rc->btc', latent, w_ukv, preferred_element_type=jnp.float32).astype(jnp.bfloat16)
    kv_up = kv_up.reshape(n_prompts, seq_len, n_heads, nope_dim + v_dim)
    k_nope = kv_up[..., :nope_dim]
    values = kv_up[..., nope_dim:]
    score_scale = (nope_dim + rope_dim) ** -0.5
    scores = jnp.einsum('bqhd,bkhd->bhqk', q_nope, k_nope, preferred_element_type=jnp.float32)
    scores = scores + jnp.einsum('crie,cle->cirl', q_pe, k_pe, preferred_element_type=jnp.float32)
    causal = jnp.arange(seq_len)[:, None] >= jnp.arange(seq_len)[None, :]
    scores = jnp.where(causal, scores * score_scale, -1e30)
    attn_probs = jax.nn.softmax(scores, axis=-1).astype(jnp.bfloat16)
    attn_out = jnp.einsum('bhqk,bkhd->bqhd', attn_probs, values, preferred_element_type=jnp.float32).astype(jnp.bfloat16)
    attn_out = attn_out.reshape(n_prompts, seq_len, n_heads * v_dim)
    return jnp.einsum('btc,cd->btd', attn_out, w_out, preferred_element_type=jnp.float32)


def attend_each(q_lat, latent, k_pe, w_uq, w_ukv, w_out, head_info, cos_t, sin_t):
    def one_prompt(operands):
        q_one, lat_one, pe_one = operands
        return attend(q_one[None], lat_one[None], pe_one[None], w_uq, w_ukv, w_out, head_info, cos_t, sin_t)[0]

    return lax.map(one_prompt, (q_lat, latent, k_pe))


def solution(mesh):
    batch_spec = P(('dp', 'fsdp'))
    row_spec = P('fsdp')
    mat_spec = P('fsdp', None)

    def run_block(tokens, gain_in, w_dq, gain_q, w_uq, w_dkv, gain_kv, w_ukv, w_out):
        head_info = head_dims(w_uq, w_dkv, gain_kv, w_ukv, w_out)
        seq_len = tokens.shape[1]

        def local_block(tok_blk, gain_in_s, w_dq_s, gain_q_s, w_uq_s, w_dkv_s, gain_kv_s, w_ukv_s, w_out_s):
            cos_t, sin_t = rope_tables(seq_len, head_info[2])
            gain_in_all = lax.all_gather(gain_in_s, 'fsdp', tiled=True)
            w_dq_all = lax.all_gather(w_dq_s, 'fsdp', tiled=True)
            gain_q_all = lax.all_gather(gain_q_s, 'fsdp', tiled=True)
            w_dkv_all = lax.all_gather(w_dkv_s, 'fsdp', tiled=True)
            gain_kv_all = lax.all_gather(gain_kv_s, 'fsdp', tiled=True)
            q_lat, latent, k_pe = latents(tok_blk, gain_in_all, w_dq_all, gain_q_all, w_dkv_all, gain_kv_all, cos_t, sin_t)
            w_uq_all = lax.all_gather(w_uq_s, 'fsdp', tiled=True)
            w_ukv_all = lax.all_gather(w_ukv_s, 'fsdp', tiled=True)
            w_out_all = lax.all_gather(w_out_s, 'fsdp', tiled=True)
            proj_out = attend_each(q_lat, latent, k_pe, w_uq_all, w_ukv_all, w_out_all, head_info, cos_t, sin_t)
            y_blk = (tok_blk.astype(jnp.float32) + proj_out).astype(jnp.bfloat16)
            return y_blk, latent, k_pe

        mapped = jax.shard_map(
            local_block,
            mesh=mesh,
            in_specs=(batch_spec, row_spec, mat_spec, row_spec, mat_spec, mat_spec, row_spec, mat_spec, mat_spec),
            out_specs=(batch_spec, batch_spec, batch_spec),
            check_vma=False,
        )
        return mapped(tokens, gain_in, w_dq, gain_q, w_uq, w_dkv, gain_kv, w_ukv, w_out)

    return run_block
```

profile of v0, /device:TPU:88, one launch (start us, length us, event | category | flops | bytes accessed | tf_op | source)
XLA Modules:
  0.0 441.7 jit_solution(16372457086802667263)
XLA Ops:
  14.2 16.4 %all-reduce.3 = (bf16[2560]{0:T(1024)(128)(2,1)S(1)}, bf16[256]{0:T(256)(128)(2,1)S(1)}, bf16[768]{0:T(1024)(128)(2,1)S(1)}) all-reduce(bf16[2560]{0:T(1024)(128)(2,1)S(1)} %dynamic-update-slice, bf16[256]{0:T(256)(128)(2,1)S(1)} %dynamic-update-slice.1, bf16[768]{0:T(1024)(128)(2,1)S(1)} %dynamic-update-slice.2), channel_id=1, replica_groups=mesh['dp'=4,'fsdp'=8] {'fsdp'}, use_global_device_ids=true, to_apply=%add | all-reduce | flops 3584 | bytes 14336
  30.7 6.1 %fusion.29 = f32[16,128]{1,0:T(8,128)S(1)} fusion(bf16[16,128,2560]{2,1,0:T(8,128)(2,1)} %param.11), kind=kLoop, calls=%fused_computation.43 | loop fusion | flops 15726592 | bytes 10493952 | tf_op jit(solution)/shard_map/reduce_sum | solution.py:12
  41.4 6.6 %fusion.35 = f32[16,128,288]{1,2,0:T(8,128)S(1)} fusion(bf16[2560,288,1]{0,1,2:T(8,128)(2,1)} %reshape.199, bf16[16,128,2560]{2,1,0:T(8,128)(2,1)} %param.11, f32[2560]{0:T(1024)S(1)} %convert_element_type.48, f32[16,128]{1,0:T(8,128)S(1)} %add_rsqrt_fusion.2), kind=kOutput, calls=%fused_computation.48 | convolution fusion | flops 3040870400 | bytes 14338048 | tf_op jit(solution)/shard_map/btd,dr->btr/dot_general | solution.py:42
  49.8 13.7 %all-gather.9.cloned.1.call-done = bf16[2560,768]{1,0:T(8,128)(2,1)} async-done(((bf16[320,768]{1,0:T(8,128)(2,1)}), bf16[2560,768]{1,0:T(8,128)(2,1)}) %all-gather.9.cloned.1.call-update) | async-done | bytes 3932176 | tf_op jit(solution)/shard_map/all_gather | solution.py:91
  63.5 12.5 %multiply_reduce_fusion = (f32[16,128]{1,0:T(8,128)S(1)}, f32[16,128,768]{2,1,0:T(8,128)S(1)}) fusion(bf16[2560,768]{1,0:T(8,128)(2,1)} %all-gather.9.cloned.1.call-done, bf16[16,128,2560]{2,1,0:T(8,128)(2,1)} %param.11, f32[2560]{0:T(1024)S(1)} %convert_element_type.48, f32[16,128]{1,0:T(8,128)S(1)} %add_rsqrt_fusion.2), kind=kOutput, calls=%fused_computation.50 | convolution fusion | flops 8077178880 | bytes 20736000 | tf_op jit(solution)/shard_map/btd,dr->btr/dot_general | solution.py:40
  78.3 22.6 %all-gather.11.cloned.1.call-done = bf16[768,3840]{1,0:T(8,128)(2,1)} async-done(((bf16[96,3840]{1,0:T(8,128)(2,1)}), bf16[768,3840]{1,0:T(8,128)(2,1)}) %all-gather.11.cloned.1.call-update) | async-done | bytes 5898256 | tf_op jit(solution)/shard_map/all_gather | solution.py:96
  100.9 8.4 %copy.24 = bf16[768,3840]{0,1:T(8,128)(2,1)} copy(bf16[768,3840]{1,0:T(8,128)(2,1)} %all-gather.11.cloned.1.call-done) | data formatting | bytes 11796480
  109.3 16.1 %all-gather.7.cloned.1.call-done = bf16[256,5120]{1,0:T(8,128)(2,1)} async-done(((bf16[32,5120]{1,0:T(8,128)(2,1)}), bf16[256,5120]{1,0:T(8,128)(2,1)}) %all-gather.7.cloned.1.call-update) | async-done | bytes 2621456 | tf_op jit(solution)/shard_map/all_gather | solution.py:97
  125.5 68.5 %all-gather.13.cloned.1.call-done = bf16[2560,2560]{1,0:T(8,128)(2,1)} async-done(((bf16[320,2560]{1,0:T(8,128)(2,1)}), bf16[2560,2560]{1,0:T(8,128)(2,1)}) %all-gather.13.cloned.1.call-update) | async-done | bytes 13107216 | tf_op jit(solution)/shard_map/all_gather | solution.py:98
  193.9 225.6 %while.13 = (s32[]{:T(128)}, f32[16,128,2560]{2,1,0:T(8,128)}, bf16[16,128,256]{2,1,0:T(8,128)(2,1)}, bf16[256,5120]{1,0:T(8,128)(2,1)}, bf16[16,128,768]{2,1,0:...) while((s32[]{:T(128)}, f32[16,128,2560]{2,1,0:T(8,128)}, ...), condition=%wide.region_6.7_spmd.clone.clone.clone, body=%wide.region_3.6_spmd.clone.clone.clone.sunk | while | flops 2986156032 | bytes 86292232 | solution.py:76
  197.0 4.7 %convolution_bitcast_fusion.3 = f32[1,128,40,96]{1,3,2,0:T(8,128)S(1)} fusion(bf16[40,96,768]{2,1,0:T(8,128)(2,1)} %bitcast.106, bf16[16,128,768]{2,1,0:T(8,128)(2,1)} %get-tuple-element.285, s32[]{:T(128)} %get-tuple-element.271), kind=kOutput, calls=%fused_computation.11.clone.1 | convolution fusion | flops 754974720 | bytes 8061440 | tf_op jit(solution)/shard_map/while/body/eval_jaxpr/btr,rc->btc/dot_general | solution.py:52
  225.2 4.7 %convolution_bitcast_fusion.3 = f32[1,128,40,96]{1,3,2,0:T(8,128)S(1)} fusion(bf16[40,96,768]{2,1,0:T(8,128)(2,1)} %bitcast.106, bf16[16,128,768]{2,1,0:T(8,128)(2,1)} %get-tuple-element.285, s32[]{:T(128)} %get-tuple-element.271), kind=kOutput, calls=%fused_computation.11.clone.1 | convolution fusion | flops 754974720 | bytes 8061440 | tf_op jit(solution)/shard_map/while/body/eval_jaxpr/btr,rc->btc/dot_general | solution.py:52
  239.3 4.7 %convolution_bitcast_fusion.3 = f32[1,128,40,96]{1,3,2,0:T(8,128)S(1)} fusion(bf16[40,96,768]{2,1,0:T(8,128)(2,1)} %bitcast.106, bf16[16,128,768]{2,1,0:T(8,128)(2,1)} %get-tuple-element.285, s32[]{:T(128)} %get-tuple-element.271), kind=kOutput, calls=%fused_computation.11.clone.1 | convolution fusion | flops 754974720 | bytes 8061440 | tf_op jit(solution)/shard_map/while/body/eval_jaxpr/btr,rc->btc/dot_general | solution.py:52
  253.4 4.7 %convolution_bitcast_fusion.3 = f32[1,128,40,96]{1,3,2,0:T(8,128)S(1)} fusion(bf16[40,96,768]{2,1,0:T(8,128)(2,1)} %bitcast.106, bf16[16,128,768]{2,1,0:T(8,128)(2,1)} %get-tuple-element.285, s32[]{:T(128)} %get-tuple-element.271), kind=kOutput, calls=%fused_computation.11.clone.1 | convolution fusion | flops 754974720 | bytes 8061440 | tf_op jit(solution)/shard_map/while/body/eval_jaxpr/btr,rc->btc/dot_general | solution.py:52
  267.5 4.7 %convolution_bitcast_fusion.3 = f32[1,128,40,96]{1,3,2,0:T(8,128)S(1)} fusion(bf16[40,96,768]{2,1,0:T(8,128)(2,1)} %bitcast.106, bf16[16,128,768]{2,1,0:T(8,128)(2,1)} %get-tuple-element.285, s32[]{:T(128)} %get-tuple-element.271), kind=kOutput, calls=%fused_computation.11.clone.1 | convolution fusion | flops 754974720 | bytes 8061440 | tf_op jit(solution)/shard_map/while/body/eval_jaxpr/btr,rc->btc/dot_general | solution.py:52
  281.6 4.7 %convolution_bitcast_fusion.3 = f32[1,128,40,96]{1,3,2,0:T(8,128)S(1)} fusion(bf16[40,96,768]{2,1,0:T(8,128)(2,1)} %bitcast.106, bf16[16,128,768]{2,1,0:T(8,128)(2,1)} %get-tuple-element.285, s32[]{:T(128)} %get-tuple-element.271), kind=kOutput, calls=%fused_computation.11.clone.1 | convolution fusion | flops 754974720 | bytes 8061440 | tf_op jit(solution)/shard_map/while/body/eval_jaxpr/btr,rc->btc/dot_general | solution.py:52
  295.8 4.7 %convolution_bitcast_fusion.3 = f32[1,128,40,96]{1,3,2,0:T(8,128)S(1)} fusion(bf16[40,96,768]{2,1,0:T(8,128)(2,1)} %bitcast.106, bf16[16,128,768]{2,1,0:T(8,128)(2,1)} %get-tuple-element.285, s32[]{:T(128)} %get-tuple-element.271), kind=kOutput, calls=%fused_computation.11.clone.1 | convolution fusion | flops 754974720 | bytes 8061440 | tf_op jit(solution)/shard_map/while/body/eval_jaxpr/btr,rc->btc/dot_general | solution.py:52
  323.9 4.7 %convolution_bitcast_fusion.3 = f32[1,128,40,96]{1,3,2,0:T(8,128)S(1)} fusion(bf16[40,96,768]{2,1,0:T(8,128)(2,1)} %bitcast.106, bf16[16,128,768]{2,1,0:T(8,128)(2,1)} %get-tuple-element.285, s32[]{:T(128)} %get-tuple-element.271), kind=kOutput, calls=%fused_computation.11.clone.1 | convolution fusion | flops 754974720 | bytes 8061440 | tf_op jit(solution)/shard_map/while/body/eval_jaxpr/btr,rc->btc/dot_general | solution.py:52
  338.1 4.7 %convolution_bitcast_fusion.3 = f32[1,128,40,96]{1,3,2,0:T(8,128)S(1)} fusion(bf16[40,96,768]{2,1,0:T(8,128)(2,1)} %bitcast.106, bf16[16,128,768]{2,1,0:T(8,128)(2,1)} %get-tuple-element.285, s32[]{:T(128)} %get-tuple-element.271), kind=kOutput, calls=%fused_computation.11.clone.1 | convolution fusion | flops 754974720 | bytes 8061440 | tf_op jit(solution)/shard_map/while/body/eval_jaxpr/btr,rc->btc/dot_general | solution.py:52
  352.2 4.7 %convolution_bitcast_fusion.3 = f32[1,128,40,96]{1,3,2,0:T(8,128)S(1)} fusion(bf16[40,96,768]{2,1,0:T(8,128)(2,1)} %bitcast.106, bf16[16,128,768]{2,1,0:T(8,128)(2,1)} %get-tuple-element.285, s32[]{:T(128)} %get-tuple-element.271), kind=kOutput, calls=%fused_computation.11.clone.1 | convolution fusion | flops 754974720 | bytes 8061440 | tf_op jit(solution)/shard_map/while/body/eval_jaxpr/btr,rc->btc/dot_general | solution.py:52
  380.3 4.7 %convolution_bitcast_fusion.3 = f32[1,128,40,96]{1,3,2,0:T(8,128)S(1)} fusion(bf16[40,96,768]{2,1,0:T(8,128)(2,1)} %bitcast.106, bf16[16,128,768]{2,1,0:T(8,128)(2,1)} %get-tuple-element.285, s32[]{:T(128)} %get-tuple-element.271), kind=kOutput, calls=%fused_computation.11.clone.1 | convolution fusion | flops 754974720 | bytes 8061440 | tf_op jit(solution)/shard_map/while/body/eval_jaxpr/btr,rc->btc/dot_general | solution.py:52
  394.4 4.7 %convolution_bitcast_fusion.3 = f32[1,128,40,96]{1,3,2,0:T(8,128)S(1)} fusion(bf16[40,96,768]{2,1,0:T(8,128)(2,1)} %bitcast.106, bf16[16,128,768]{2,1,0:T(8,128)(2,1)} %get-tuple-element.285, s32[]{:T(128)} %get-tuple-element.271), kind=kOutput, calls=%fused_computation.11.clone.1 | convolution fusion | flops 754974720 | bytes 8061440 | tf_op jit(solution)/shard_map/while/body/eval_jaxpr/btr,rc->btc/dot_general | solution.py:52
  408.5 4.7 %convolution_bitcast_fusion.3 = f32[1,128,40,96]{1,3,2,0:T(8,128)S(1)} fusion(bf16[40,96,768]{2,1,0:T(8,128)(2,1)} %bitcast.106, bf16[16,128,768]{2,1,0:T(8,128)(2,1)} %get-tuple-element.285, s32[]{:T(128)} %get-tuple-element.271), kind=kOutput, calls=%fused_computation.11.clone.1 | convolution fusion | flops 754974720 | bytes 8061440 | tf_op jit(solution)/shard_map/while/body/eval_jaxpr/btr,rc->btc/dot_general | solution.py:52
  419.5 15.7 %fusion.32 = bf16[16,128,2560]{2,1,0:T(8,128)(2,1)} fusion(f32[16,128,2560]{2,1,0:T(8,128)} %get-tuple-element.61, bf16[16,128,2560]{2,1,0:T(8,128)(2,1)} %param.11), kind=kLoop, calls=%fused_computation.46 | loop fusion | flops 15728640 | bytes 41943040 | tf_op jit(solution)/shard_map/convert_element_type | solution.py:100
  (352 shorter events, 176.9 us)
Async XLA Ops:
  7.2 29.7 %all-gather.15.cloned.1.call-start = ((), (), s32[]{:S(2)}) async-start(), calls=%async_computation.4 | async-start | bytes 1990656 | tf_op jit(solution)/shard_map/all_gather | solution.py:93
  8.0 55.5 %all-gather.9.cloned.1.call-start = ((), (), s32[]{:S(2)}) async-start(), calls=%async_computation.1 | async-start | bytes 4423680 | tf_op jit(solution)/shard_map/all_gather | solution.py:91
  8.8 92.1 %all-gather.11.cloned.1.call-start = ((), (), s32[]{:S(2)}) async-start(), calls=%async_computation.2 | async-start | bytes 6635520 | tf_op jit(solution)/shard_map/all_gather | solution.py:96
  9.6 115.8 %all-gather.7.cloned.1.call-start = ((), (), s32[]{:S(2)}) async-start(), calls=%async_computation | async-start | bytes 2949120 | tf_op jit(solution)/shard_map/all_gather | solution.py:97
  10.3 183.7 %all-gather.13.cloned.1.call-start = ((), (), s32[]{:S(2)}) async-start(), calls=%async_computation.3 | async-start | bytes 14745600 | tf_op jit(solution)/shard_map/all_gather | solution.py:98
  211.1 7.3 %slice-start = ((s8[13107200]{0:T(1024)(128)(4,1)}), s8[4194304]{0:T(1024)(128)(4,1)S(1)}, s32[]{:S(2)}) async-start(s8[13107200]{0:T(1024)(128)(4,1)} %bitcast.104), calls=%async_computation.5 | async-start | bytes 8388608 | tf_op jit(solution)/shard_map/while
  211.1 7.3 %slice-start.1 = ((s8[13107200]{0:T(1024)(128)(4,1)}), s8[4194304]{0:T(1024)(128)(4,1)S(1)}, s32[]{:S(2)}) async-start(s8[13107200]{0:T(1024)(128)(4,1)} %bitcast.104), calls=%async_computation.6 | async-start | bytes 8388608 | tf_op jit(solution)/shard_map/while
  225.2 7.3 %slice-start = ((s8[13107200]{0:T(1024)(128)(4,1)}), s8[4194304]{0:T(1024)(128)(4,1)S(1)}, s32[]{:S(2)}) async-start(s8[13107200]{0:T(1024)(128)(4,1)} %bitcast.104), calls=%async_computation.5 | async-start | bytes 8388608 | tf_op jit(solution)/shard_map/while
  225.2 7.3 %slice-start.1 = ((s8[13107200]{0:T(1024)(128)(4,1)}), s8[4194304]{0:T(1024)(128)(4,1)S(1)}, s32[]{:S(2)}) async-start(s8[13107200]{0:T(1024)(128)(4,1)} %bitcast.104), calls=%async_computation.6 | async-start | bytes 8388608 | tf_op jit(solution)/shard_map/while
  253.4 7.3 %slice-start = ((s8[13107200]{0:T(1024)(128)(4,1)}), s8[4194304]{0:T(1024)(128)(4,1)S(1)}, s32[]{:S(2)}) async-start(s8[13107200]{0:T(1024)(128)(4,1)} %bitcast.104), calls=%async_computation.5 | async-start | bytes 8388608 | tf_op jit(solution)/shard_map/while
  253.4 7.3 %slice-start.1 = ((s8[13107200]{0:T(1024)(128)(4,1)}), s8[4194304]{0:T(1024)(128)(4,1)S(1)}, s32[]{:S(2)}) async-start(s8[13107200]{0:T(1024)(128)(4,1)} %bitcast.104), calls=%async_computation.6 | async-start | bytes 8388608 | tf_op jit(solution)/shard_map/while
  267.5 7.3 %slice-start = ((s8[13107200]{0:T(1024)(128)(4,1)}), s8[4194304]{0:T(1024)(128)(4,1)S(1)}, s32[]{:S(2)}) async-start(s8[13107200]{0:T(1024)(128)(4,1)} %bitcast.104), calls=%async_computation.5 | async-start | bytes 8388608 | tf_op jit(solution)/shard_map/while
  267.5 7.3 %slice-start.1 = ((s8[13107200]{0:T(1024)(128)(4,1)}), s8[4194304]{0:T(1024)(128)(4,1)S(1)}, s32[]{:S(2)}) async-start(s8[13107200]{0:T(1024)(128)(4,1)} %bitcast.104), calls=%async_computation.6 | async-start | bytes 8388608 | tf_op jit(solution)/shard_map/while
  281.6 7.3 %slice-start = ((s8[13107200]{0:T(1024)(128)(4,1)}), s8[4194304]{0:T(1024)(128)(4,1)S(1)}, s32[]{:S(2)}) async-start(s8[13107200]{0:T(1024)(128)(4,1)} %bitcast.104), calls=%async_computation.5 | async-start | bytes 8388608 | tf_op jit(solution)/shard_map/while
  281.6 7.3 %slice-start.1 = ((s8[13107200]{0:T(1024)(128)(4,1)}), s8[4194304]{0:T(1024)(128)(4,1)S(1)}, s32[]{:S(2)}) async-start(s8[13107200]{0:T(1024)(128)(4,1)} %bitcast.104), calls=%async_computation.6 | async-start | bytes 8388608 | tf_op jit(solution)/shard_map/while
  295.8 7.3 %slice-start = ((s8[13107200]{0:T(1024)(128)(4,1)}), s8[4194304]{0:T(1024)(128)(4,1)S(1)}, s32[]{:S(2)}) async-start(s8[13107200]{0:T(1024)(128)(4,1)} %bitcast.104), calls=%async_computation.5 | async-start | bytes 8388608 | tf_op jit(solution)/shard_map/while
  295.8 7.3 %slice-start.1 = ((s8[13107200]{0:T(1024)(128)(4,1)}), s8[4194304]{0:T(1024)(128)(4,1)S(1)}, s32[]{:S(2)}) async-start(s8[13107200]{0:T(1024)(128)(4,1)} %bitcast.104), calls=%async_computation.6 | async-start | bytes 8388608 | tf_op jit(solution)/shard_map/while
  338.1 7.3 %slice-start = ((s8[13107200]{0:T(1024)(128)(4,1)}), s8[4194304]{0:T(1024)(128)(4,1)S(1)}, s32[]{:S(2)}) async-start(s8[13107200]{0:T(1024)(128)(4,1)} %bitcast.104), calls=%async_computation.5 | async-start | bytes 8388608 | tf_op jit(solution)/shard_map/while
  338.1 7.3 %slice-start.1 = ((s8[13107200]{0:T(1024)(128)(4,1)}), s8[4194304]{0:T(1024)(128)(4,1)S(1)}, s32[]{:S(2)}) async-start(s8[13107200]{0:T(1024)(128)(4,1)} %bitcast.104), calls=%async_computation.6 | async-start | bytes 8388608 | tf_op jit(solution)/shard_map/while
  352.2 7.3 %slice-start = ((s8[13107200]{0:T(1024)(128)(4,1)}), s8[4194304]{0:T(1024)(128)(4,1)S(1)}, s32[]{:S(2)}) async-start(s8[13107200]{0:T(1024)(128)(4,1)} %bitcast.104), calls=%async_computation.5 | async-start | bytes 8388608 | tf_op jit(solution)/shard_map/while
  352.2 7.3 %slice-start.1 = ((s8[13107200]{0:T(1024)(128)(4,1)}), s8[4194304]{0:T(1024)(128)(4,1)S(1)}, s32[]{:S(2)}) async-start(s8[13107200]{0:T(1024)(128)(4,1)} %bitcast.104), calls=%async_computation.6 | async-start | bytes 8388608 | tf_op jit(solution)/shard_map/while
  408.5 7.3 %slice-start = ((s8[13107200]{0:T(1024)(128)(4,1)}), s8[4194304]{0:T(1024)(128)(4,1)S(1)}, s32[]{:S(2)}) async-start(s8[13107200]{0:T(1024)(128)(4,1)} %bitcast.104), calls=%async_computation.5 | async-start | bytes 8388608 | tf_op jit(solution)/shard_map/while
  408.5 7.3 %slice-start.1 = ((s8[13107200]{0:T(1024)(128)(4,1)}), s8[4194304]{0:T(1024)(128)(4,1)S(1)}, s32[]{:S(2)}) async-start(s8[13107200]{0:T(1024)(128)(4,1)} %bitcast.104), calls=%async_computation.6 | async-start | bytes 8388608 | tf_op jit(solution)/shard_map/while
  419.5 15.7 %copy-start = (bf16[16,128,32]{1,2,0:T(8,128)(2,1)}, bf16[16,128,32]{1,2,0:T(8,128)(2,1)S(1)}, u32[]{:S(2)}) copy-start(bf16[16,128,32]{1,2,0:T(8,128)(2,1)S(1)} %get-tuple-element.309) | copy-start | bytes 393220
  (50 other events, 181.6 us)
Sparse Core Ops, SparseCore 0:
  9.6 24.4 all-gather.14
  35.8 27.7 all-gather.8
  65.1 35.7 all-gather.10
  102.3 23.0 all-gather.6
  126.9 66.9 all-gather.12
where the time goes:
time: 445 us; the launch traced here: 442 us
  matrix products  206 us (46%)
  waiting for transfers between devices  124 us (28%)
  local copies, waits for them, and re-layouts  40 us (9%)
  other arithmetic  36.9 us (8%)
  blocking collectives  16.4 us (4%)
  between operations  15.9 us (4%)
    dot_general x16, matrix products, attend(): jnp.einsum('btr,rc->btc', q_lat, w_uq, preferred_element_type=jnp.float32)  74.5 us
    all_gather x1, waiting for transfers between devices, local_block(): w_out_all = lax.all_gather(w_out_s, 'fsdp', tiled=True)  68.5 us
    dot_general x16, matrix products, attend(): jnp.einsum('btc,cd->btd', attn_out, w_out, preferred_element_type=jnp.flo...  47.8 us
    dot_general x16, matrix products, attend(): jnp.einsum('btr,rc->btc', latent, w_ukv, preferred_element_type=jnp.float32)  36.7 us
    all_gather x1, waiting for transfers between devices, local_block(): w_uq_all = lax.all_gather(w_uq_s, 'fsdp', tiled=True)  22.6 us
    unnamed x1, blocking collectives  16.4 us
    all_gather x1, waiting for transfers between devices, local_block(): w_ukv_all = lax.all_gather(w_ukv_s, 'fsdp', tiled=True)  16.1 us
    convert_element_type x1, other arithmetic, local_block(): y_blk = (tok_blk.astype(jnp.float32) + proj_out).astype(jnp.bfloat16)  15.7 us
  transfers between devices with their start and end apart: 5, of which 4 were waited for; matrix products, arithmetic and copies ran while one was open for 10% of the time, Pallas kernels for 0%

commit v1 on v0

v1 whole, which is shorter than its diff:
```python
import functools
import math

import jax
import jax.numpy as jnp
from jax import lax
from jax.experimental import pallas as pl
from jax.experimental.pallas import tpu as pltpu
from jax.sharding import PartitionSpec as P

EPSILON = 1e-6
ROPE_THETA = 10000.0
BF16 = jnp.bfloat16
F32 = jnp.float32
MESH = pl.DeviceIdType.MESH

SPLIT = {320: (112, 96), 96: (32, 32), 32: (16, 0)}
N_KINDS = 11
GROUPS = 5
DQ_CUTS = 3
OUT_CUTS = 5
BLOCK = 256


def rope_tables(seq_len, rope_dim):
    half_dim = rope_dim // 2
    inv_freq = ROPE_THETA ** (-2.0 * jnp.arange(half_dim, dtype=F32) / rope_dim)
    angles = jnp.arange(seq_len, dtype=F32)[:, None] * inv_freq[None, :]
    return jnp.cos(angles), jnp.sin(angles)


def nt_dot(lhs, rhs):
    return lax.dot_general(lhs, rhs, (((1,), (1,)), ((), ())), preferred_element_type=F32)


class Piece:
    def __init__(self, base, src, dst, rows):
        self.base, self.src, self.dst, self.rows = base, src, dst, rows
        self.m, self.c = SPLIT[rows]


def gather_kernel(dims, x_hbm, gains_hbm, dq_hbm, uq_hbm, dkv_hbm, ukv_hbm, out_hbm,
                  cos_r, sin_lo, sin_hi, cos_t, sin_t,
                  o_hbm, lat_hbm, pe_hbm, wout_hbm,
                  gains_all, w_dkv, w_dq, w_uq, w_ukv, w_out,
                  a_buf, qd_buf, cq_buf, lat_buf, pe_buf, rcomb, x_buf, wqt, qf, o_blk,
                  send_sem, recv_sem, own_sem, gain_send, gain_recv, x_sem, o_sem, fin_sem):
    n_fsdp, seq_len, kv_rank, rope_dim, nope, v_dim, heads_per_group = dims
    half = rope_dim // 2
    head_q = nope + rope_dim
    n_tok, d_model = a_buf.shape
    n_blk = n_tok // BLOCK
    q_rank = cq_buf.shape[1]
    me = lax.axis_index('fsdp')
    dp = lax.axis_index('dp')
    n_x = n_fsdp // 2
    core = me % 2
    xx = me // 2
    right = ((xx + 1) % n_x) * 2 + core
    left = ((xx + n_x - 1) % n_x) * 2 + core
    far = ((xx + 2) % n_x) * 2 + core
    mate = xx * 2 + 1 - core
    par = dp % 2
    dp_mate = dp + 1 - 2 * par

    barrier = pltpu.get_barrier_semaphore()
    for k in range(1, n_fsdp):
        pl.semaphore_signal(barrier, inc=1, device_id={'fsdp': (me + k) % n_fsdp}, device_id_type=MESH)
    pl.semaphore_signal(barrier, inc=1, device_id={'dp': dp_mate}, device_id_type=MESH)

    def x_copy(blk, slot):
        return pltpu.make_async_copy(x_hbm.at[pl.ds(blk * BLOCK, BLOCK), :], x_buf.at[slot], x_sem.at[slot])

    x_copy(0, 0).start()

    def rows_of(ref, owner, rows, off, count, cols=None):
        start = pl.multiple_of(owner * rows + off, 16)
        return ref.at[pl.ds(start, count), :]

    pieces = {}
    base = [0]

    def add(unit, src, dst, rows):
        pieces.setdefault(unit, []).append(Piece(base[0], src, dst, rows))
        base[0] += 1

    add(0, dkv_hbm, w_dkv, dkv_hbm.shape[0])
    cut = q_rank // DQ_CUTS
    for j in range(DQ_CUTS):
        add(1 + j, dq_hbm.at[:, pl.ds(j * cut, cut)], w_dq.at[j], dq_hbm.shape[0])
    uq_cols, ukv_cols = heads_per_group * head_q, heads_per_group * (nope + v_dim)
    for g in range(GROUPS):
        add(1 + DQ_CUTS + g, uq_hbm.at[:, pl.ds(g * uq_cols, uq_cols)], w_uq.at[g], uq_hbm.shape[0])
        add(1 + DQ_CUTS + g, ukv_hbm.at[:, pl.ds(g * ukv_cols, ukv_cols)], w_ukv.at[g], ukv_hbm.shape[0])
    out_cols = out_hbm.shape[1] // OUT_CUTS
    for j in range(OUT_CUTS):
        add(1 + DQ_CUTS + GROUPS + j, out_hbm.at[:, pl.ds(j * out_cols, out_cols)], w_out.at[j], out_hbm.shape[0])
    n_units = 1 + DQ_CUTS + GROUPS + OUT_CUTS

    def copy(p, kind, owner, off, count, to, from_own=False):
        start = pl.multiple_of(off, 16) if not isinstance(off, int) else off
        dst = rows_of(p.dst, owner, p.rows, off, count)
        src = p.src.at[pl.ds(start, count), :] if from_own else dst
        return pltpu.make_async_remote_copy(
            src_ref=src, dst_ref=dst, send_sem=send_sem.at[p.base, kind], recv_sem=recv_sem.at[p.base, kind],
            device_id=to, device_id_type=MESH)

    def geom(p):
        edge = p.rows - p.m - p.c
        x_off = par * edge
        m_off = par * (p.rows - p.m)
        z_off = (1 - par) * (p.rows - p.m)
        return x_off, m_off, z_off

    to_right, to_left, to_mate, to_dp = {'fsdp': right}, {'fsdp': left}, {'fsdp': mate}, {'dp': dp_mate}
    mate_of = lambda owner: owner + 1 - 2 * core

    def own_copy(p):
        return pltpu.make_async_copy(p.src, rows_of(p.dst, me, p.rows, 0, p.rows), own_sem.at[p.base])

    def start_own(unit):
        for p in pieces[unit]:
            x_off, _, _ = geom(p)
            copy(p, 0, me, x_off, p.m + p.c, to_right, True).start()
            copy(p, 1, me, x_off, p.m + p.c, to_left, True).start()
            copy(p, 7, me, 0, p.rows, to_mate, True).start()
            own_copy(p).start()

    def stage1(unit):
        for p in pieces[unit]:
            x_off, m_off, _ = geom(p)
            copy(p, 0, left, x_off, p.m + p.c, to_right).wait_recv()
            copy(p, 2, left, m_off, p.m, to_right).start()
            copy(p, 4, left, m_off, p.m, to_dp).start()
            copy(p, 1, right, x_off, p.m + p.c, to_left).wait_recv()
            if p.c:
                copy(p, 3, right, p.m, p.c, to_left).start()
            copy(p, 5, right, m_off, p.m, to_dp).start()

    def stage2(unit):
        for p in pieces[unit]:
            _, m_off, _ = geom(p)
            copy(p, 2, far, m_off, p.m, to_right).wait_recv()
            copy(p, 6, far, m_off, p.m, to_dp).start()
            if p.c:
                copy(p, 3, far, p.m, p.c, to_left).wait_recv()

    def stage3(unit):
        for p in pieces[unit]:
            _, _, z_off = geom(p)
            for kind, owner in ((4, left), (5, right), (6, far)):
                copy(p, kind, owner, z_off, p.m, to_dp).wait_recv()
                copy(p, kind + 4, owner, 0, p.rows, to_mate).start()

    def stage4(unit):
        for p in pieces[unit]:
            for kind, owner in ((7, me), (8, left), (9, right), (10, far)):
                copy(p, kind, mate_of(owner), 0, p.rows, to_mate).wait_recv()
            own_copy(p).wait()

    def all_sent(unit):
        for p in pieces[unit]:
            x_off, m_off, _ = geom(p)
            copy(p, 0, me, x_off, p.m + p.c, to_right, True).wait_send()
            copy(p, 1, me, x_off, p.m + p.c, to_left, True).wait_send()
            copy(p, 2, left, m_off, p.m, to_right).wait_send()
            if p.c:
                copy(p, 3, right, p.m, p.c, to_left).wait_send()
            for kind, owner in ((4, left), (5, right), (6, far)):
                copy(p, kind, owner, m_off, p.m, to_dp).wait_send()
            copy(p, 7, me, 0, p.rows, to_mate, True).wait_send()
            for kind, owner in ((8, left), (9, right), (10, far)):
                copy(p, kind, owner, 0, p.rows, to_mate).wait_send()

    pl.semaphore_wait(barrier, n_fsdp)

    def gain_copy(k, owner):
        return pltpu.make_async_remote_copy(
            src_ref=gains_hbm, dst_ref=gains_all.at[owner], send_sem=gain_send.at[k], recv_sem=gain_recv.at[k],
            device_id={'fsdp': (me + k) % n_fsdp}, device_id_type=MESH)

    own_gain = pltpu.make_async_copy(gains_hbm, gains_all.at[me], gain_recv.at[0])
    own_gain.start()
    for k in range(1, n_fsdp):
        gain_copy(k, me).start()
    start_own(0)
    start_own(1)
    own_gain.wait()
    for k in range(1, n_fsdp):
        gain_copy(k, (me + n_fsdp - k) % n_fsdp).wait_recv()

    gains = gains_all[0]
    for k in range(1, n_fsdp):
        gains = gains + gains_all[k]
    g_rows = d_model // 128
    q_rows = q_rank // 128
    kv_rows = kv_rank // 128

    def norm_step(blk, carry):
        slot = blk % 2

        @pl.when(blk + 1 < n_blk)
        def _():
            x_copy(blk + 1, (blk + 1) % 2).start()

        x_copy(blk, slot).wait()
        row0 = pl.multiple_of(blk * BLOCK, BLOCK)
        for r in range(0, BLOCK, 32):
            xb = x_buf[slot, r:r + 32, :].astype(F32)
            inv = lax.rsqrt(jnp.sum(xb * xb, axis=-1, keepdims=True) * (1.0 / d_model) + EPSILON)
            for j in range(g_rows):
                a_buf[pl.ds(row0 + r, 32), j * 128:(j + 1) * 128] = (
                    xb[:, j * 128:(j + 1) * 128] * inv * gains[j:j + 1, :]).astype(BF16)
        return carry

    lax.fori_loop(0, n_blk, norm_step, 0)

    def tick_a(t):
        stage1(t)
        if t + 2 < n_units:
            start_own(t + 2)

    def tick_b(t):
        if 0 <= t - 1 < n_units:
            stage2(t - 1)
        if 0 <= t - 2 < n_units:
            stage3(t - 2)
        if 0 <= t - 3 < n_units:
            stage4(t - 3)

    for t in range(4):
        tick_a(t)
        tick_b(t)

    def lat_step(blk, carry):
        row0 = pl.multiple_of(blk * BLOCK, BLOCK)
        rows = pl.ds(row0, BLOCK)
        u = jnp.dot(a_buf[rows, :], w_dkv[...], preferred_element_type=F32)
        lat = u[:, :kv_rank]
        inv = lax.rsqrt(jnp.sum(lat * lat, axis=-1, keepdims=True) * (1.0 / kv_rank) + EPSILON)
        for j in range(kv_rows):
            lat_buf[rows, j * 128:(j + 1) * 128] = (
                lat[:, j * 128:(j + 1) * 128] * inv * gains[g_rows + q_rows + j:g_rows + q_rows + j + 1, :]).astype(BF16)
        pe = jnp.concatenate([u[:, kv_rank:], jnp.zeros((BLOCK, 128 - rope_dim), F32)], axis=-1)
        cs = jnp.concatenate([cos_r[...]] * (BLOCK // seq_len), axis=0)
        lo = jnp.concatenate([sin_lo[...]] * (BLOCK // seq_len), axis=0)
        hi = jnp.concatenate([sin_hi[...]] * (BLOCK // seq_len), axis=0)
        rot = pe * cs - pltpu.roll(pe, 128 - half, 1) * lo + pltpu.roll(pe, half, 1) * hi
        rot = rot.astype(BF16)
        pe_buf[rows, :] = rot[:, :rope_dim]
        rcomb[rows, :] = pltpu.roll(rot.astype(F32), nope, 1)
        return carry

    lax.fori_loop(0, n_blk, lat_step, 0)
    lat_out = pltpu.make_async_copy(lat_buf, lat_hbm, fin_sem.at[0])
    pe_out = pltpu.make_async_copy(pe_buf, pe_hbm, fin_sem.at[1])
    lat_out.start()
    pe_out.start()

    def qd_cut(j):
        def qd_step(blk, carry):
            rows = pl.ds(pl.multiple_of(blk * BLOCK, BLOCK), BLOCK)
            qd_buf[rows, j * cut:(j + 1) * cut] = jnp.dot(a_buf[rows, :], w_dq[j], preferred_element_type=F32)
            return carry

        lax.fori_loop(0, n_blk, qd_step, 0)

    for j in range(DQ_CUTS):
        tick_a(4 + j)
        tick_b(4 + j)
        qd_cut(j)

    def cq_step(blk, carry):
        rows = pl.ds(pl.multiple_of(blk * BLOCK, BLOCK), BLOCK)
        qd = qd_buf[rows, :]
        inv = lax.rsqrt(jnp.sum(qd * qd, axis=-1, keepdims=True) * (1.0 / q_rank) + EPSILON)
        for j in range(q_rows):
            cq_buf[rows, j * 128:(j + 1) * 128] = (
                qd[:, j * 128:(j + 1) * 128] * inv * gains[g_rows + j:g_rows + j + 1, :]).astype(BF16)
        return carry

    lax.fori_loop(0, n_blk, cq_step, 0)
    t_first = 4 + DQ_CUTS
    tick_a(t_first)
    tick_b(t_first)

    n_steps = GROUPS * n_blk
    span = n_blk // 2 + 1
    schedule = {}
    last = n_units + 2
    for i, t in enumerate(range(t_first + 1, last + 1)):
        if 5 * i + 1 < n_steps:
            schedule.setdefault(5 * i, []).append(functools.partial(tick_a, t) if t < n_units else None)
            schedule.setdefault(5 * i + 2, []).append(functools.partial(tick_b, t))
            done_tick = t
    n_pairs = heads_per_group // 2
    scale = head_q ** -0.5
    c2 = scale * math.log2(math.e)
    mask_val = -1e30 / scale

    def o_copy(g, row0, slot):
        return pltpu.make_async_copy(
            o_blk.at[slot], o_hbm.at[pl.ds(row0, BLOCK), pl.ds(pl.multiple_of(g * heads_per_group * v_dim, 128),
                                                              heads_per_group * v_dim)], o_sem.at[slot])

    def attn_step(step, carry):
        g = step // n_blk
        blk = step % n_blk
        slot = step % 2
        row0 = pl.multiple_of(blk * BLOCK, BLOCK)
        rows = pl.ds(row0, BLOCK)
        for at, fns in schedule.items():
            if any(fn is not None for fn in fns):
                @pl.when(step == at)
                def _():
                    for fn in fns:
                        if fn is not None:
                            fn()

        @pl.when(blk == 0)
        def _():
            for j in range(uq_cols // 128):
                wqt[j * 128:(j + 1) * 128, :] = w_uq[g, :, j * 128:(j + 1) * 128].T

        @pl.when(step >= 2)
        def _():
            o_copy(0, 0, slot).wait()

        qf[...] = nt_dot(wqt[...], cq_buf[rows, :])
        kvf = jnp.dot(lat_buf[rows, :], w_ukv[g], preferred_element_type=F32)
        lane = lax.broadcasted_iota(jnp.int32, (BLOCK, 128), 1)
        keep = lax.broadcasted_iota(jnp.int32, (seq_len, seq_len), 0) <= lax.broadcasted_iota(
            jnp.int32, (seq_len, seq_len), 1)
        ct, st = cos_t[...], sin_t[...]
        rc = rcomb[rows, :]
        for pair in range(n_pairs):
            outs = [[], []]
            for h in (2 * pair, 2 * pair + 1):
                q0 = h * head_q
                v1 = qf[q0 + nope:q0 + nope + half, :]
                v2 = qf[q0 + nope + half:q0 + head_q, :]
                q_aug = jnp.concatenate([
                    qf[q0:q0 + nope, :].astype(BF16),
                    (v1 * ct - v2 * st).astype(BF16),
                    (v2 * ct + v1 * st).astype(BF16),
                    jnp.zeros((128 - head_q, BLOCK), BF16)], axis=0)
                kvh = kvf[:, h * 128:(h + 1) * 128]
                k_aug = jnp.where(lane < nope, kvh, rc).astype(BF16)
                v_t = kvh.astype(BF16).T[nope:, :]
                for p in range(BLOCK // seq_len):
                    tok = slice(p * seq_len, (p + 1) * seq_len)
                    s_t = jnp.dot(k_aug[tok, :], q_aug[:, tok], preferred_element_type=F32)
                    s_t = jnp.where(keep, s_t, mask_val)
                    top = jnp.max(s_t, axis=0, keepdims=True)
                    e_t = jnp.exp2((s_t - top) * c2)
                    tot = jnp.sum(e_t, axis=0, keepdims=True)
                    p_t = (e_t * (1.0 / tot)).astype(BF16)
                    outs[p].append(jnp.dot(v_t[:, tok], p_t, preferred_element_type=F32))
            for p in range(BLOCK // seq_len):
                both = jnp.concatenate(outs[p], axis=0).astype(BF16)
                o_blk[slot, p * seq_len:(p + 1) * seq_len, pair * 128:(pair + 1) * 128] = both.T
        o_copy(g, row0, slot).start()
        return carry

    lax.fori_loop(0, n_steps, attn_step, 0)

    for t in range(done_tick + 1, last + 1):
        if t < n_units:
            tick_a(t)
        tick_b(t)
    outs = []
    for j in range(OUT_CUTS):
        cp = pltpu.make_async_copy(w_out.at[j], wout_hbm.at[:, pl.ds(j * out_cols, out_cols)], fin_sem.at[2 + j])
        cp.start()
        outs.append(cp)
    for slot in range(2):
        o_copy(0, 0, slot).wait()
    lat_out.wait()
    pe_out.wait()
    for unit in range(n_units):
        all_sent(unit)
    for k in range(1, n_fsdp):
        gain_copy(k, me).wait_send()
    for cp in outs:
        cp.wait()


def attention_part(x, gains, dq_s, uq_s, dkv_s, ukv_s, out_s, n_fsdp, seq_len, q_rank, kv_rank):
    n_tok, d_model = x.shape
    rope_dim = dkv_s.shape[1] - kv_rank
    v_total = out_s.shape[0] * n_fsdp
    nope_total = ukv_s.shape[1] - v_total
    n_heads = (uq_s.shape[1] - nope_total) // rope_dim
    nope, v_dim = nope_total // n_heads, v_total // n_heads
    hpg = n_heads // GROUPS
    half = rope_dim // 2
    cos_s, sin_s = rope_tables(seq_len, rope_dim)
    pad = jnp.zeros((seq_len, 128 - rope_dim), F32)
    zero = jnp.zeros((seq_len, half), F32)
    cos_r = jnp.concatenate([cos_s, cos_s, pad], axis=1)
    sin_lo = jnp.concatenate([sin_s, zero, pad], axis=1)
    sin_hi = jnp.concatenate([zero, sin_s, pad], axis=1)
    reps = BLOCK // seq_len
    cos_t = jnp.concatenate([cos_s.T] * reps, axis=1)
    sin_t = jnp.concatenate([sin_s.T] * reps, axis=1)
    dims = (n_fsdp, seq_len, kv_rank, rope_dim, nope, v_dim, hpg)
    n_pieces = 1 + DQ_CUTS + 2 * GROUPS + OUT_CUTS
    any_spec = pl.BlockSpec(memory_space=pl.ANY)
    vmem_spec = pl.BlockSpec(memory_space=pltpu.VMEM)
    dma = pltpu.SemaphoreType.DMA
    return pl.pallas_call(
        functools.partial(gather_kernel, dims),
        out_shape=(
            jax.ShapeDtypeStruct((n_tok, v_total), BF16),
            jax.ShapeDtypeStruct((n_tok, kv_rank), BF16),
            jax.ShapeDtypeStruct((n_tok, rope_dim), BF16),
            jax.ShapeDtypeStruct((v_total, d_model), BF16),
        ),
        in_specs=[any_spec] * 7 + [vmem_spec] * 5,
        out_specs=(any_spec,) * 4,
        scratch_shapes=[
            pltpu.VMEM((n_fsdp,) + gains.shape, F32),
            pltpu.VMEM((dkv_s.shape[0] * n_fsdp, dkv_s.shape[1]), BF16),
            pltpu.VMEM((DQ_CUTS, d_model, q_rank // DQ_CUTS), BF16),
            pltpu.VMEM((GROUPS, q_rank, uq_s.shape[1] // GROUPS), BF16),
            pltpu.VMEM((GROUPS, kv_rank, ukv_s.shape[1] // GROUPS), BF16),
            pltpu.VMEM((OUT_CUTS, v_total, d_model // OUT_CUTS), BF16),
            pltpu.VMEM((n_tok, d_model), BF16),
            pltpu.VMEM((n_tok, q_rank), F32),
            pltpu.VMEM((n_tok, q_rank), BF16),
            pltpu.VMEM((n_tok, kv_rank), BF16),
            pltpu.VMEM((n_tok, rope_dim), BF16),
            pltpu.VMEM((n_tok, 128), F32),
            pltpu.VMEM((2, BLOCK, d_model), BF16),
            pltpu.VMEM((hpg * (nope + rope_dim), q_rank), BF16),
            pltpu.VMEM((hpg * (nope + rope_dim), BLOCK), F32),
            pltpu.VMEM((2, BLOCK, hpg * v_dim), BF16),
            dma((n_pieces, N_KINDS)),
            dma((n_pieces, N_KINDS)),
            dma((n_pieces,)),
            dma((n_fsdp,)),
            dma((n_fsdp,)),
            dma((2,)),
            dma((2,)),
            dma((2 + OUT_CUTS,)),
        ],
        compiler_params=pltpu.CompilerParams(
            collective_id=0, has_side_effects=True, vmem_limit_bytes=67043328),
        name='latent_attention',
    )(x, gains, dq_s, uq_s, dkv_s, ukv_s, out_s, cos_r, sin_lo, sin_hi, cos_t, sin_t)


def solution(mesh):
    batch_spec = P(('dp', 'fsdp'))
    row_spec = P('fsdp')
    mat_spec = P('fsdp', None)
    n_fsdp = mesh.shape['fsdp']

    def run_block(tokens, gain_in, w_dq, gain_q, w_uq, w_dkv, gain_kv, w_ukv, w_out):
        seq_len = tokens.shape[1]

        def local_block(tok_blk, g_in, dq_s, g_q, uq_s, dkv_s, g_kv, ukv_s, out_s):
            n_prompts, _, d_model = tok_blk.shape
            me = lax.axis_index('fsdp')
            total = (g_in.shape[0] + g_q.shape[0] + g_kv.shape[0]) * n_fsdp
            rows = -(-total // 1024) * 8
            flat = jnp.zeros((rows * 128,), F32)
            start = 0
            for gain in (g_in, g_q, g_kv):
                flat = lax.dynamic_update_slice(flat, gain.astype(F32), (start + me * gain.shape[0],))
                start += gain.shape[0] * n_fsdp
            gains = flat.reshape(rows, 128)
            x = tok_blk.reshape(n_prompts * seq_len, d_model)
            attn_out, latent, k_pe, w_out_all = attention_part(
                x, gains, dq_s, uq_s, dkv_s, ukv_s, out_s, n_fsdp, seq_len, g_q.shape[0] * n_fsdp,
                g_kv.shape[0] * n_fsdp)
            proj = jnp.dot(attn_out, w_out_all, preferred_element_type=F32)
            y = (x.astype(F32) + proj).astype(BF16)
            return (y.reshape(tok_blk.shape), latent.reshape(n_prompts, seq_len, -1),
                    k_pe.reshape(n_prompts, seq_len, -1))

        mapped = jax.shard_map(
            local_block,
            mesh=mesh,
            in_specs=(batch_spec, row_spec, mat_spec, row_spec, mat_spec, mat_spec, row_spec, mat_spec, mat_spec),
            out_specs=(batch_spec, batch_spec, batch_spec),
            check_vma=False,
        )
        return mapped(tokens, gain_in, w_dq, gain_q, w_uq, w_dkv, gain_kv, w_ukv, w_out)

    return run_block
```

time: 445 us -> 260 us (0.58)
  Pallas kernels: 0 us -> 216 us
  matrix products: 206 us -> 35.2 us
  waiting for transfers between devices: 124 us -> 0 us
  local copies, waits for them, and re-layouts: 40 us -> 3.69 us
  other arithmetic: 36.9 us -> 4 us
  blocking collectives: 16.4 us -> 0 us
  between operations: 15.9 us -> 0.7 us
    pallas_call x0 -> x1, Pallas kernels: none -> 216 us  [attention_part(): pl.pallas_call(functools.partial(gather_kernel, dims), out_shape=(jax.Sha...]
    dot_general x98 -> x1, matrix products: 206 us -> 35.2 us  [local_block(): proj = jnp.dot(attn_out, w_out_all, preferred_element_type=F32)]
    all_gather x5 -> x0, waiting for transfers between devices: 121 us -> none  [the longest x1 68.5 us: local_block(): w_out_all = lax.all_gather(w_out_s, 'fsdp', tiled=True)]
    convert_element_type x6 -> x0, other arithmetic: 18.2 us -> none  [the longest x1 15.7 us: local_block(): y_blk = (tok_blk.astype(jnp.float32) + proj_out).astype(jnp.bfloat16)]
    unnamed x1 -> x0, blocking collectives: 16.4 us -> none
    reduce_sum x18 -> x0, other arithmetic: 14.8 us -> none  [the longest x16 8.58 us: attend(): attn_probs = jax.nn.softmax(scores, axis=-1).astype(jnp.bfloat16)]
    reshape x16 -> x0, local copies, waits for them, and re-layouts: 12.5 us -> none  [attend(): kv_up = kv_up.reshape(n_prompts, seq_len, n_heads, nope_dim + v_dim)]
    while x128 -> x0, local copies, waits for them, and re-layouts: 12 us -> none
  transfers between devices with their start and end apart: 5 -> 0, of which waited for: 4 -> 0; matrix products, arithmetic and copies ran while one was open for 10% -> 0% of each run, Pallas kernels for 0% -> 0%
where the time goes in v1:
time: 260 us
  Pallas kernels  216 us (83%)
  matrix products  35.2 us (14%)
  other arithmetic  4 us (2%)
  local copies, waits for them, and re-layouts  3.69 us (1%)
    pallas_call x1, Pallas kernels, attention_part(): pl.pallas_call(functools.partial(gather_kernel, dims), out_shape=(jax.Sha...  216 us
    dot_general x1, matrix products, local_block(): proj = jnp.dot(attn_out, w_out_all, preferred_element_type=F32)  35.2 us

profile of v1, /device:TPU:88, one launch (start us, length us, event | category | flops | bytes accessed | tf_op | source)
XLA Modules:
  0.0 259.5 jit_solution(11100981106273952811)
XLA Ops:
  0.7 0.1 pad.12.clone
  0.7 0.8 convert_dynamic-update-slice_fusion
  1.5 0.7 convert_dynamic-update-slice_fusion.2
  2.2 0.7 convert_dynamic-update-slice_fusion.1
  3.0 0.0 copy-start.2
  3.0 0.1 fusion.2
  3.1 0.6 pad_maximum_fusion
  3.7 0.0 copy-done.2
  3.7 0.3 fusion
  4.0 0.8 maximum_maximum_fusion.2
  4.8 1.8 copy.12.dkv_hbm
  6.5 215.9 %latent_attention.1 = (bf16[2048,2560]{1,0:T(8,128)(2,1)}, bf16[2048,256]{1,0:T(8,128)(2,1)}, bf16[2048,32]{1,0:T(8,128)(2,1)}, bf16[2560,2560]{1,0:T(8,128)(2,1)}) custom-call(bf16[2048,2560]{1,0:T(8,128)(2,1)} %bitcast.7, f32[32,128]{1,0:T(8,128)} %bitcast.11, bf16[320,768]{1,0:T(8,128)(2,1)} %dq_hbm.1, bf16[96,3840]{1,0:T(8,128)(2,1)} %uq_hbm.1, ...), custom_call_target="tpu_custom_call" | custom-call | tf_op jit(solution)/shard_map/latent_attention/pallas_call | solution.py:411
  222.5 0.0 copy-start.1
  222.5 0.0 copy-start
  222.5 35.2 %add_convert_fusion = bf16[2048,2560]{1,0:T(8,128)(2,1)} fusion(bf16[2048,2560]{1,0:T(8,128)(2,1)} %bitcast.8, bf16[2048,2560]{1,0:T(8,128)(2,1)} %get-tuple-element.7, bf16[2560,2560]{1,0:T(8,128)(2,1)} %get-tuple-element.8), kind=kOutput, calls=%fused_computation | convolution fusion | flops 26859274240 | bytes 44564480 | tf_op jit(solution)/shard_map/dot_general | solution.py:477
  257.7 0.0 copy-done.1
  257.7 0.8 copy.13
  258.6 0.0 copy-done
  258.6 1.0 copy.18
  (4 shorter events, 0.0 us)
Async XLA Ops:
  3.0 0.7 copy-start.2
  222.5 35.2 %copy-start.1 = (bf16[2048,32]{1,0:T(8,128)(2,1)S(1)}, bf16[2048,32]{1,0:T(8,128)(2,1)}, u32[]{:S(2)}) copy-start(bf16[2048,32]{1,0:T(8,128)(2,1)} %get-tuple-element.10) | copy-start | bytes 393220
  222.5 36.1 %copy-start = (bf16[2048,256]{1,0:T(8,128)(2,1)S(1)}, bf16[2048,256]{1,0:T(8,128)(2,1)}, u32[]{:S(2)}) copy-start(bf16[2048,256]{1,0:T(8,128)(2,1)} %get-tuple-element.9) | copy-start | bytes 3145732

commit v2 on v1

--- a/solution.py
+++ b/solution.py
@@ -43,7 +43,7 @@
                   cos_r, sin_lo, sin_hi, cos_t, sin_t,
                   o_hbm, lat_hbm, pe_hbm, wout_hbm,
                   gains_all, w_dkv, w_dq, w_uq, w_ukv, w_out,
-                  a_buf, qd_buf, cq_buf, lat_buf, pe_buf, rcomb, x_buf, wqt, qf, o_blk,
+                  a_buf, qd_buf, cq_buf, lat_buf, pe_buf, rcomb, u_buf, wqt, wk, wvt, qf, kf, vt, sbuf, o_blk,
                   send_sem, recv_sem, own_sem, gain_send, gain_recv, x_sem, o_sem, fin_sem):
     n_fsdp, seq_len, kv_rank, rope_dim, nope, v_dim, heads_per_group = dims
     half = rope_dim // 2
@@ -68,10 +68,12 @@
         pl.semaphore_signal(barrier, inc=1, device_id={'fsdp': (me + k) % n_fsdp}, device_id_type=MESH)
     pl.semaphore_signal(barrier, inc=1, device_id={'dp': dp_mate}, device_id_type=MESH)
 
-    def x_copy(blk, slot):
-        return pltpu.make_async_copy(x_hbm.at[pl.ds(blk * BLOCK, BLOCK), :], x_buf.at[slot], x_sem.at[slot])
-
-    x_copy(0, 0).start()
+    def x_copy(blk):
+        rows = pl.ds(pl.multiple_of(blk * BLOCK, BLOCK), BLOCK)
+        return pltpu.make_async_copy(x_hbm.at[rows, :], a_buf.at[rows, :], x_sem.at[blk])
+
+    for blk in range(n_blk):
+        x_copy(blk).start()
 
     def rows_of(ref, owner, rows, off, count, cols=None):
         start = pl.multiple_of(owner * rows + off, 16)
@@ -189,86 +191,130 @@
     for k in range(1, n_fsdp):
         gain_copy(k, (me + n_fsdp - k) % n_fsdp).wait_recv()
 
-    gains = gains_all[0]
-    for k in range(1, n_fsdp):
-        gains = gains + gains_all[k]
+    lane_row = lax.broadcasted_iota(jnp.int32, (1, 128), 1)
+    gain_rows = [None] * ((d_model + q_rank + kv_rank) // 128)
+
+    def put(row, value):
+        gain_rows[row] = value if gain_rows[row] is None else gain_rows[row] + value
+
+    for owner in range(n_fsdp):
+        base_row, local_row = 0, 0
+        for total in (d_model, q_rank, kv_rank):
+            count = total // n_fsdp
+            for r in range(-(-count // 128)):
+                size = min(128, count - 128 * r)
+                at = owner * count + 128 * r
+                row, off = base_row + at // 128, at % 128
+                value = gains_all[owner, local_row:local_row + 1, :]
+                if off:
+                    value = pltpu.roll(value, off, 1)
+                    put(row, jnp.where(lane_row >= off, value, 0.0))
+                    if off + size > 128:
+                        put(row + 1, jnp.where(lane_row < off, value, 0.0))
+                else:
+                    put(row, value)
+                local_row += 1
+            base_row += total // 128
+    gains = jnp.concatenate(gain_rows, axis=0)
     g_rows = d_model // 128
     q_rows = q_rank // 128
     kv_rows = kv_rank // 128
 
     def norm_step(blk, carry):
-        slot = blk % 2
-
-        @pl.when(blk + 1 < n_blk)
-        def _():
-            x_copy(blk + 1, (blk + 1) % 2).start()
-
-        x_copy(blk, slot).wait()
+        x_copy(blk).wait()
         row0 = pl.multiple_of(blk * BLOCK, BLOCK)
         for r in range(0, BLOCK, 32):
-            xb = x_buf[slot, r:r + 32, :].astype(F32)
+            xb = a_buf[pl.ds(row0 + r, 32), :].astype(F32)
             inv = lax.rsqrt(jnp.sum(xb * xb, axis=-1, keepdims=True) * (1.0 / d_model) + EPSILON)
             for j in range(g_rows):
                 a_buf[pl.ds(row0 + r, 32), j * 128:(j + 1) * 128] = (
                     xb[:, j * 128:(j + 1) * 128] * inv * gains[j:j + 1, :]).astype(BF16)
         return carry
 
-    lax.fori_loop(0, n_blk, norm_step, 0)
-
     def tick_a(t):
         stage1(t)
         if t + 2 < n_units:
             start_own(t + 2)
 
-    def tick_b(t):
-        if 0 <= t - 1 < n_units:
-            stage2(t - 1)
-        if 0 <= t - 2 < n_units:
-            stage3(t - 2)
-        if 0 <= t - 3 < n_units:
-            stage4(t - 3)
-
-    for t in range(4):
-        tick_a(t)
-        tick_b(t)
-
     def lat_step(blk, carry):
-        row0 = pl.multiple_of(blk * BLOCK, BLOCK)
-        rows = pl.ds(row0, BLOCK)
-        u = jnp.dot(a_buf[rows, :], w_dkv[...], preferred_element_type=F32)
-        lat = u[:, :kv_rank]
+        rows = pl.ds(pl.multiple_of(blk * 2 * BLOCK, BLOCK), 2 * BLOCK)
+        u_buf[rows, :] = jnp.dot(a_buf[rows, :], w_dkv[...], preferred_element_type=F32)
+        return carry
+
+    def lat_finish(blk):
+        rows = pl.ds(pl.multiple_of(blk * BLOCK, BLOCK), BLOCK)
+        lat = u_buf[rows, :kv_rank]
         inv = lax.rsqrt(jnp.sum(lat * lat, axis=-1, keepdims=True) * (1.0 / kv_rank) + EPSILON)
         for j in range(kv_rows):
             lat_buf[rows, j * 128:(j + 1) * 128] = (
                 lat[:, j * 128:(j + 1) * 128] * inv * gains[g_rows + q_rows + j:g_rows + q_rows + j + 1, :]).astype(BF16)
-        pe = jnp.concatenate([u[:, kv_rank:], jnp.zeros((BLOCK, 128 - rope_dim), F32)], axis=-1)
+        pe = jnp.concatenate([u_buf[rows, kv_rank:], jnp.zeros((BLOCK, 128 - rope_dim), F32)], axis=-1)
         cs = jnp.concatenate([cos_r[...]] * (BLOCK // seq_len), axis=0)
         lo = jnp.concatenate([sin_lo[...]] * (BLOCK // seq_len), axis=0)
         hi = jnp.concatenate([sin_hi[...]] * (BLOCK // seq_len), axis=0)
         rot = pe * cs - pltpu.roll(pe, 128 - half, 1) * lo + pltpu.roll(pe, half, 1) * hi
         rot = rot.astype(BF16)
         pe_buf[rows, :] = rot[:, :rope_dim]
-        rcomb[rows, :] = pltpu.roll(rot.astype(F32), nope, 1)
-        return carry
-
-    lax.fori_loop(0, n_blk, lat_step, 0)
+        rcomb[rows, :] = rot
+
+    def run(fn, lo, hi):
+        lax.fori_loop(lo, hi, fn, 0)
+
+    run(norm_step, 0, 6)
+    tick_a(0)
+    run(norm_step, 6, n_blk)
+    tick_a(1)
+    stage2(0)
+    tick_a(2)
+    stage2(1)
+    stage3(0)
+    tick_a(3)
+    stage4(0)
+    stage2(2)
+    half_blk = n_blk // 2
+    run(lat_step, 0, 1)
+    stage3(1)
+    run(lat_step, 1, 2)
+    tick_a(4)
+    stage2(3)
+    run(lat_step, 2, 3)
+    stage3(2)
+    run(lat_step, 3, half_blk)
+    tick_a(5)
+    def qd_cut(j, lo, hi):
+        def qd_step(blk, carry):
+            rows = pl.ds(pl.multiple_of(blk * 2 * BLOCK, BLOCK), 2 * BLOCK)
+            qd_buf[rows, j * cut:(j + 1) * cut] = jnp.dot(a_buf[rows, :], w_dq[j], preferred_element_type=F32)
+            if j == 0:
+                lat_finish(2 * blk)
+                lat_finish(2 * blk + 1)
+            return carry
+
+        lax.fori_loop(lo, hi, qd_step, 0)
+
+    mid = half_blk // 2
+    stage2(4)
+    stage4(1)
+    qd_cut(0, 0, mid)
+    stage3(3)
+    qd_cut(0, mid, half_blk)
     lat_out = pltpu.make_async_copy(lat_buf, lat_hbm, fin_sem.at[0])
     pe_out = pltpu.make_async_copy(pe_buf, pe_hbm, fin_sem.at[1])
     lat_out.start()
     pe_out.start()
 
-    def qd_cut(j):
-        def qd_step(blk, carry):
-            rows = pl.ds(pl.multiple_of(blk * BLOCK, BLOCK), BLOCK)
-            qd_buf[rows, j * cut:(j + 1) * cut] = jnp.dot(a_buf[rows, :], w_dq[j], preferred_element_type=F32)
-            return carry
-
-        lax.fori_loop(0, n_blk, qd_step, 0)
-
-    for j in range(DQ_CUTS):
-        tick_a(4 + j)
-        tick_b(4 + j)
-        qd_cut(j)
+    tick_a(6)
+    stage4(2)
+    qd_cut(1, 0, mid)
+    stage2(5)
+    qd_cut(1, mid, half_blk)
+    stage3(4)
+    stage4(3)
+    qd_cut(2, 0, mid)
+    tick_a(7)
+    qd_cut(2, mid, half_blk)
+    stage2(6)
+    stage3(5)
 
     def cq_step(blk, carry):
         rows = pl.ds(pl.multiple_of(blk * BLOCK, BLOCK), BLOCK)
@@ -280,19 +326,28 @@
         return carry
 
     lax.fori_loop(0, n_blk, cq_step, 0)
-    t_first = 4 + DQ_CUTS
-    tick_a(t_first)
-    tick_b(t_first)
+    stage4(4)
 
     n_steps = GROUPS * n_blk
-    span = n_blk // 2 + 1
+
+    def out_copy(j):
+        return pltpu.make_async_copy(w_out.at[j], wout_hbm.at[:, pl.ds(j * out_cols, out_cols)], fin_sem.at[2 + j])
+
+    first_out = 1 + DQ_CUTS + GROUPS
+
+    def finish_out(unit):
+        stage4(unit)
+        out_copy(unit - first_out).start()
+
+    plan = [(0, tick_a, 8), (1, stage2, 7), (1, stage3, 6), (3, stage2, 8), (4, stage3, 7), (5, tick_a, 9),
+            (7, stage3, 8), (8, stage4, 5), (8, stage2, 9), (10, tick_a, 10), (12, stage3, 9), (13, stage2, 10),
+            (15, tick_a, 11), (15, finish_out, 9), (16, stage4, 6), (17, stage3, 10), (18, stage2, 11),
+            (20, tick_a, 12), (20, finish_out, 10), (22, stage3, 11), (23, stage2, 12), (24, stage4, 7),
+            (25, tick_a, 13), (25, finish_out, 11), (27, stage3, 12), (28, stage2, 13), (30, finish_out, 12),
+            (32, stage4, 8), (33, stage3, 13), (36, finish_out, 13)]
     schedule = {}
-    last = n_units + 2
-    for i, t in enumerate(range(t_first + 1, last + 1)):
-        if 5 * i + 1 < n_steps:
-            schedule.setdefault(5 * i, []).append(functools.partial(tick_a, t) if t < n_units else None)
-            schedule.setdefault(5 * i + 2, []).append(functools.partial(tick_b, t))
-            done_tick = t
+    for at, fn, unit in plan:
+        schedule.setdefault(at, []).append((fn, unit))
     n_pairs = heads_per_group // 2
     scale = head_q ** -0.5
     c2 = scale * math.log2(math.e)
@@ -309,70 +364,84 @@
         slot = step % 2
         row0 = pl.multiple_of(blk * BLOCK, BLOCK)
         rows = pl.ds(row0, BLOCK)
-        for at, fns in schedule.items():
-            if any(fn is not None for fn in fns):
-                @pl.when(step == at)
-                def _():
-                    for fn in fns:
-                        if fn is not None:
-                            fn()
+        for part in range(GROUPS):
+            @pl.when(g == part)
+            def _():
+                for at, todo in schedule.items():
+                    if at // n_blk == part:
+                        @pl.when(step == at)
+                        def _():
+                            for fn, unit in todo:
+                                fn(unit)
 
         @pl.when(blk == 0)
         def _():
             for j in range(uq_cols // 128):
                 wqt[j * 128:(j + 1) * 128, :] = w_uq[g, :, j * 128:(j + 1) * 128].T
+            low = lax.broadcasted_iota(jnp.int32, (kv_rank, 128), 1) < nope
+            for j in range(n_pairs):
+                even = w_ukv[g, :, (2 * j) * 128:(2 * j + 1) * 128].astype(F32)
+                odd = w_ukv[g, :, (2 * j + 1) * 128:(2 * j + 2) * 128].astype(F32)
+                wk[:, j * 128:(j + 1) * 128] = jnp.where(low, even, pltpu.roll(odd, nope, 1)).astype(BF16)
+                wvt[j * 128:(j + 1) * 128, :] = jnp.where(low, pltpu.roll(even, nope, 1), odd).astype(BF16).T
 
         @pl.when(step >= 2)
         def _():
             o_copy(0, 0, slot).wait()
 
-        qf[...] = nt_dot(wqt[...], cq_buf[rows, :])
-        kvf = jnp.dot(lat_buf[rows, :], w_ukv[g], preferred_element_type=F32)
-        lane = lax.broadcasted_iota(jnp.int32, (BLOCK, 128), 1)
-        keep = lax.broadcasted_iota(jnp.int32, (seq_len, seq_len), 0) <= lax.broadcasted_iota(
-            jnp.int32, (seq_len, seq_len), 1)
+        @pl.when(step < n_steps)
+        def _():
+            qf[...] = nt_dot(wqt[...], cq_buf[rows, :])
+            kf[...] = jnp.dot(lat_buf[rows, :], wk[...], preferred_element_type=F32).astype(BF16)
+            vt[...] = nt_dot(wvt[...], lat_buf[rows, :]).astype(BF16)
+
+        keep = lax.broadcasted_iota(jnp.int32, (seq_len, 2 * seq_len), 0) <= lax.broadcasted_iota(
+            jnp.int32, (seq_len, 2 * seq_len), 1) % seq_len
         ct, st = cos_t[...], sin_t[...]
         rc = rcomb[rows, :]
-        for pair in range(n_pairs):
-            outs = [[], []]
-            for h in (2 * pair, 2 * pair + 1):
-                q0 = h * head_q
-                v1 = qf[q0 + nope:q0 + nope + half, :]
-                v2 = qf[q0 + nope + half:q0 + head_q, :]
-                q_aug = jnp.concatenate([
-                    qf[q0:q0 + nope, :].astype(BF16),
-                    (v1 * ct - v2 * st).astype(BF16),
-                    (v2 * ct + v1 * st).astype(BF16),
-                    jnp.zeros((128 - head_q, BLOCK), BF16)], axis=0)
-                kvh = kvf[:, h * 128:(h + 1) * 128]
-                k_aug = jnp.where(lane < nope, kvh, rc).astype(BF16)
-                v_t = kvh.astype(BF16).T[nope:, :]
+        zero = jnp.zeros((nope, seq_len), BF16)
+        tail = jnp.zeros((128 - rope_dim, 2 * seq_len), BF16)
+        @pl.when(step < n_steps)
+        def _():
+            for pair in range(n_pairs):
+                q_nope, q_pe = [], []
+                for h in (2 * pair, 2 * pair + 1):
+                    q0 = h * head_q
+                    v1 = qf[q0 + nope:q0 + nope + half, :]
+                    v2 = qf[q0 + nope + half:q0 + head_q, :]
+                    q_nope.append(qf[q0:q0 + nope, :].astype(BF16))
+                    q_pe.append(jnp.concatenate([(v1 * ct - v2 * st).astype(BF16), (v2 * ct + v1 * st).astype(BF16)], axis=0))
+                cols = slice(pair * 128, (pair + 1) * 128)
                 for p in range(BLOCK // seq_len):
                     tok = slice(p * seq_len, (p + 1) * seq_len)
-                    s_t = jnp.dot(k_aug[tok, :], q_aug[:, tok], preferred_element_type=F32)
+                    k_all = jnp.concatenate([kf[tok, cols], rc[tok, :]], axis=1)
+                    q_all = jnp.concatenate([
+                        jnp.concatenate([q_nope[0][:, tok], zero], axis=1),
+                        jnp.concatenate([zero, q_nope[1][:, tok]], axis=1),
+                        jnp.concatenate([q_pe[0][:, tok], q_pe[1][:, tok]], axis=1),
+                        tail], axis=0)
+                    sbuf[2 * pair + p] = jnp.dot(k_all, q_all, preferred_element_type=F32)
+
+        @pl.when(step < n_steps)
+        def _():
+            for pair in range(n_pairs):
+                cols = slice(pair * 128, (pair + 1) * 128)
+                for p in range(BLOCK // seq_len):
+                    tok = slice(p * seq_len, (p + 1) * seq_len)
+                    s_t = sbuf[2 * pair + p]
                     s_t = jnp.where(keep, s_t, mask_val)
                     top = jnp.max(s_t, axis=0, keepdims=True)
                     e_t = jnp.exp2((s_t - top) * c2)
                     tot = jnp.sum(e_t, axis=0, keepdims=True)
                     p_t = (e_t * (1.0 / tot)).astype(BF16)
-                    outs[p].append(jnp.dot(v_t[:, tok], p_t, preferred_element_type=F32))
-            for p in range(BLOCK // seq_len):
-                both = jnp.concatenate(outs[p], axis=0).astype(BF16)
-                o_blk[slot, p * seq_len:(p + 1) * seq_len, pair * 128:(pair + 1) * 128] = both.T
+                    both = jnp.dot(vt[cols, tok], p_t, preferred_element_type=F32)
+                    both = jnp.concatenate([both[:v_dim, :seq_len], both[v_dim:, seq_len:]], axis=0)
+                    o_blk[slot, tok, cols] = both.astype(BF16).T
         o_copy(g, row0, slot).start()
         return carry
 
     lax.fori_loop(0, n_steps, attn_step, 0)
 
-    for t in range(done_tick + 1, last + 1):
-        if t < n_units:
-            tick_a(t)
-        tick_b(t)
-    outs = []
-    for j in range(OUT_CUTS):
-        cp = pltpu.make_async_copy(w_out.at[j], wout_hbm.at[:, pl.ds(j * out_cols, out_cols)], fin_sem.at[2 + j])
-        cp.start()
-        outs.append(cp)
     for slot in range(2):
         o_copy(0, 0, slot).wait()
     lat_out.wait()
@@ -381,8 +450,8 @@
         all_sent(unit)
     for k in range(1, n_fsdp):
         gain_copy(k, me).wait_send()
-    for cp in outs:
-        cp.wait()
+    for j in range(OUT_CUTS):
+        out_copy(j).wait()
 
 
 def attention_part(x, gains, dq_s, uq_s, dkv_s, ukv_s, out_s, n_fsdp, seq_len, q_rank, kv_rank):
@@ -430,17 +499,22 @@
             pltpu.VMEM((n_tok, q_rank), BF16),
             pltpu.VMEM((n_tok, kv_rank), BF16),
             pltpu.VMEM((n_tok, rope_dim), BF16),
-            pltpu.VMEM((n_tok, 128), F32),
-            pltpu.VMEM((2, BLOCK, d_model), BF16),
+            pltpu.VMEM((n_tok, 128), BF16),
+            pltpu.VMEM((n_tok, dkv_s.shape[1]), F32),
             pltpu.VMEM((hpg * (nope + rope_dim), q_rank), BF16),
+            pltpu.VMEM((kv_rank, hpg * nope), BF16),
+            pltpu.VMEM((hpg * v_dim, kv_rank), BF16),
             pltpu.VMEM((hpg * (nope + rope_dim), BLOCK), F32),
+            pltpu.VMEM((BLOCK, hpg * nope), BF16),
+            pltpu.VMEM((hpg * v_dim, BLOCK), BF16),
+            pltpu.VMEM((hpg, 128, 256), F32),
             pltpu.VMEM((2, BLOCK, hpg * v_dim), BF16),
             dma((n_pieces, N_KINDS)),
             dma((n_pieces, N_KINDS)),
             dma((n_pieces,)),
             dma((n_fsdp,)),
             dma((n_fsdp,)),
-            dma((2,)),
+            dma((n_tok // BLOCK,)),
             dma((2,)),
             dma((2 + OUT_CUTS,)),
         ],
@@ -461,15 +535,9 @@
 
         def local_block(tok_blk, g_in, dq_s, g_q, uq_s, dkv_s, g_kv, ukv_s, out_s):
             n_prompts, _, d_model = tok_blk.shape
-            me = lax.axis_index('fsdp')
-            total = (g_in.shape[0] + g_q.shape[0] + g_kv.shape[0]) * n_fsdp
-            rows = -(-total // 1024) * 8
-            flat = jnp.zeros((rows * 128,), F32)
-            start = 0
-            for gain in (g_in, g_q, g_kv):
-                flat = lax.dynamic_update_slice(flat, gain.astype(F32), (start + me * gain.shape[0],))
-                start += gain.shape[0] * n_fsdp
-            gains = flat.reshape(rows, 128)
+            parts = [jnp.pad(g.astype(F32), (0, -g.shape[0] % 128)) for g in (g_in, g_q, g_kv)]
+            flat = jnp.concatenate(parts)
+            gains = jnp.pad(flat, (0, -flat.shape[0] % 1024)).reshape(-1, 128)
             x = tok_blk.reshape(n_prompts * seq_len, d_model)
             attn_out, latent, k_pe, w_out_all = attention_part(
                 x, gains, dq_s, uq_s, dkv_s, ukv_s, out_s, n_fsdp, seq_len, g_q.shape[0] * n_fsdp,

time: 260 us -> 168 us (0.65)
  Pallas kernels: 216 us -> 125 us
    pallas_call x1, Pallas kernels: 216 us -> 125 us  [attention_part(): pl.pallas_call(functools.partial(gather_kernel, dims), out_shape=(jax.Sha...]
where the time goes in v2:
time: 168 us; the launch traced here: 167 us
  Pallas kernels  125 us (74%)
  matrix products  35 us (21%)
  local copies, waits for them, and re-layouts  3.69 us (2%)
  other arithmetic  3.09 us (2%)
    pallas_call x1, Pallas kernels, attention_part(): pl.pallas_call(functools.partial(gather_kernel, dims), out_shape=(jax.Sha...  125 us
    dot_general x1, matrix products, local_block(): proj = jnp.dot(attn_out, w_out_all, preferred_element_type=F32)  35 us
    unnamed x7, local copies, waits for them, and re-layouts  3.6 us

profile of v2, /device:TPU:88, one launch (start us, length us, event | category | flops | bytes accessed | tf_op | source)
XLA Modules:
  0.0 167.4 jit_solution(17475487206572606742)
XLA Ops:
  0.7 0.1 pad.36.clone
  0.7 0.7 fusion.9
  1.5 0.6 bitcast_convert_fusion.gains_hbm
  2.0 0.1 fusion.2
  2.2 0.6 pad_maximum_fusion
  2.8 0.3 fusion
  3.1 0.8 maximum_maximum_fusion.2
  3.8 1.8 %copy.12.dkv_hbm = bf16[320,288]{1,0:T(8,128)(2,1)} copy(bf16[320,288]{0,1:T(8,128)(2,1)} %param.14) | data formatting | bytes 368640 | tf_op args[5]
  5.6 124.9 %latent_attention.1 = (bf16[2048,2560]{1,0:T(8,128)(2,1)}, bf16[2048,256]{1,0:T(8,128)(2,1)}, bf16[2048,32]{1,0:T(8,128)(2,1)}, bf16[2560,2560]{1,0:T(8,128)(2,1)}) custom-call(bf16[2048,2560]{1,0:T(8,128)(2,1)} %bitcast.9, f32[8,128]{1,0:T(8,128)} %bitcast_convert_fusion.gains_hbm, bf16[320,768]{1,0:T(8,128)(2,1)} %dq_hbm.1, bf16[96,3840]{1,0:T(8,128)(2,1)} %uq_hbm.1, ...), custom_call_target="tpu_custom_call" | custom-call | tf_op jit(solution)/shard_map/latent_attention/pallas_call | solution.py:480
  130.5 0.0 copy-start.1
  130.5 0.0 copy-start
  130.5 35.0 %add_convert_fusion = bf16[2048,2560]{1,0:T(8,128)(2,1)} fusion(bf16[2048,2560]{1,0:T(8,128)(2,1)} %bitcast.10, bf16[2048,2560]{1,0:T(8,128)(2,1)} %get-tuple-element.7, bf16[2560,2560]{1,0:T(8,128)(2,1)} %get-tuple-element.8), kind=kOutput, calls=%fused_computation | convolution fusion | flops 26859274240 | bytes 44564480 | tf_op jit(solution)/shard_map/dot_general | solution.py:545
  165.6 0.0 copy-done.1
  165.6 0.8 copy.13
  166.4 0.0 copy-done
  166.4 1.0 copy.15
  (3 shorter events, 0.0 us)
Async XLA Ops:
  130.5 35.1 %copy-start.1 = (bf16[2048,32]{1,0:T(8,128)(2,1)S(1)}, bf16[2048,32]{1,0:T(8,128)(2,1)}, u32[]{:S(2)}) copy-start(bf16[2048,32]{1,0:T(8,128)(2,1)} %get-tuple-element.10) | copy-start | bytes 393220
  130.5 35.9 %copy-start = (bf16[2048,256]{1,0:T(8,128)(2,1)S(1)}, bf16[2048,256]{1,0:T(8,128)(2,1)}, u32[]{:S(2)}) copy-start(bf16[2048,256]{1,0:T(8,128)(2,1)} %get-tuple-element.9) | copy-start | bytes 3145732

commit v3 on v2

--- a/solution.py
+++ b/solution.py
@@ -3,6 +3,7 @@
 
 import jax
 import jax.numpy as jnp
+import numpy as np
 from jax import lax
 from jax.experimental import pallas as pl
 from jax.experimental.pallas import tpu as pltpu
@@ -15,18 +16,21 @@
 MESH = pl.DeviceIdType.MESH
 
 SPLIT = {320: (112, 96), 96: (32, 32), 32: (16, 0)}
+OUT_SPLIT = (96, 128)
 N_KINDS = 11
 GROUPS = 5
 DQ_CUTS = 3
 OUT_CUTS = 5
 BLOCK = 256
+TALL = 512
+AHEAD = {12: (), 13: ()}
 
 
 def rope_tables(seq_len, rope_dim):
     half_dim = rope_dim // 2
-    inv_freq = ROPE_THETA ** (-2.0 * jnp.arange(half_dim, dtype=F32) / rope_dim)
-    angles = jnp.arange(seq_len, dtype=F32)[:, None] * inv_freq[None, :]
-    return jnp.cos(angles), jnp.sin(angles)
+    inv_freq = ROPE_THETA ** (-2.0 * np.arange(half_dim) / rope_dim)
+    angles = np.arange(seq_len)[:, None] * inv_freq[None, :]
+    return np.cos(angles).astype(np.float32), np.sin(angles).astype(np.float32)
 
 
 def nt_dot(lhs, rhs):
@@ -34,17 +38,17 @@
 
 
 class Piece:
-    def __init__(self, base, src, dst, rows):
+    def __init__(self, base, src, dst, rows, split):
         self.base, self.src, self.dst, self.rows = base, src, dst, rows
-        self.m, self.c = SPLIT[rows]
+        self.m, self.c = split or SPLIT[rows]
 
 
 def gather_kernel(dims, x_hbm, gains_hbm, dq_hbm, uq_hbm, dkv_hbm, ukv_hbm, out_hbm,
-                  cos_r, sin_lo, sin_hi, cos_t, sin_t,
+                  tab_r_hbm, tab_t_hbm,
                   o_hbm, lat_hbm, pe_hbm, wout_hbm,
-                  gains_all, w_dkv, w_dq, w_uq, w_ukv, w_out,
+                  tab_r, tab_t, gains_all, w_dkv, w_dq, w_uq, w_ukv, w_out,
                   a_buf, qd_buf, cq_buf, lat_buf, pe_buf, rcomb, u_buf, wqt, wk, wvt, qf, kf, vt, sbuf, o_blk,
-                  send_sem, recv_sem, own_sem, gain_send, gain_recv, x_sem, o_sem, fin_sem):
+                  send_sem, recv_sem, own_sem, gain_send, gain_recv, x_sem, o_sem, fin_sem, tab_sem):
     n_fsdp, seq_len, kv_rank, rope_dim, nope, v_dim, heads_per_group = dims
     half = rope_dim // 2
     head_q = nope + rope_dim
@@ -74,6 +78,12 @@
 
     for blk in range(n_blk):
         x_copy(blk).start()
+    tab_copies = (pltpu.make_async_copy(tab_r_hbm, tab_r, tab_sem.at[0]),
+                  pltpu.make_async_copy(tab_t_hbm, tab_t, tab_sem.at[1]))
+    for cp in tab_copies:
+        cp.start()
+    cos_r, sin_lo, sin_hi = tab_r.at[0], tab_r.at[1], tab_r.at[2]
+    cos_t, sin_t = tab_t.at[0], tab_t.at[1]
 
     def rows_of(ref, owner, rows, off, count, cols=None):
         start = pl.multiple_of(owner * rows + off, 16)
@@ -82,8 +92,8 @@
     pieces = {}
     base = [0]
 
-    def add(unit, src, dst, rows):
-        pieces.setdefault(unit, []).append(Piece(base[0], src, dst, rows))
+    def add(unit, src, dst, rows, split=None):
+        pieces.setdefault(unit, []).append(Piece(base[0], src, dst, rows, split))
         base[0] += 1
 
     add(0, dkv_hbm, w_dkv, dkv_hbm.shape[0])
@@ -96,7 +106,7 @@
         add(1 + DQ_CUTS + g, ukv_hbm.at[:, pl.ds(g * ukv_cols, ukv_cols)], w_ukv.at[g], ukv_hbm.shape[0])
     out_cols = out_hbm.shape[1] // OUT_CUTS
     for j in range(OUT_CUTS):
-        add(1 + DQ_CUTS + GROUPS + j, out_hbm.at[:, pl.ds(j * out_cols, out_cols)], w_out.at[j], out_hbm.shape[0])
+        add(1 + DQ_CUTS + GROUPS + j, out_hbm.at[:, pl.ds(j * out_cols, out_cols)], w_out.at[j], out_hbm.shape[0], OUT_SPLIT)
     n_units = 1 + DQ_CUTS + GROUPS + OUT_CUTS
 
     def copy(p, kind, owner, off, count, to, from_own=False):
@@ -233,11 +243,11 @@
 
     def tick_a(t):
         stage1(t)
-        if t + 2 < n_units:
-            start_own(t + 2)
+        for unit in AHEAD.get(t, (t + 2,)):
+            start_own(unit)
 
     def lat_step(blk, carry):
-        rows = pl.ds(pl.multiple_of(blk * 2 * BLOCK, BLOCK), 2 * BLOCK)
+        rows = pl.ds(pl.multiple_of(blk * TALL, TALL), TALL)
         u_buf[rows, :] = jnp.dot(a_buf[rows, :], w_dkv[...], preferred_element_type=F32)
         return carry
 
@@ -260,59 +270,63 @@
     def run(fn, lo, hi):
         lax.fori_loop(lo, hi, fn, 0)
 
-    run(norm_step, 0, 6)
+    n_tall = n_tok // TALL
+    mid = n_tall // 2
+    run(norm_step, 0, 2)
     tick_a(0)
+    run(norm_step, 2, 4)
+    tick_a(1)
+    run(norm_step, 4, 6)
+    stage2(0)
     run(norm_step, 6, n_blk)
-    tick_a(1)
-    stage2(0)
     tick_a(2)
     stage2(1)
     stage3(0)
     tick_a(3)
     stage4(0)
     stage2(2)
-    half_blk = n_blk // 2
     run(lat_step, 0, 1)
     stage3(1)
-    run(lat_step, 1, 2)
+    run(lat_step, 1, mid)
     tick_a(4)
+    run(lat_step, mid, mid + 1)
     stage2(3)
-    run(lat_step, 2, 3)
     stage3(2)
-    run(lat_step, 3, half_blk)
-    tick_a(5)
+    run(lat_step, mid + 1, n_tall)
+    for cp in tab_copies:
+        cp.wait()
     def qd_cut(j, lo, hi):
         def qd_step(blk, carry):
-            rows = pl.ds(pl.multiple_of(blk * 2 * BLOCK, BLOCK), 2 * BLOCK)
+            rows = pl.ds(pl.multiple_of(blk * TALL, TALL), TALL)
             qd_buf[rows, j * cut:(j + 1) * cut] = jnp.dot(a_buf[rows, :], w_dq[j], preferred_element_type=F32)
             if j == 0:
-                lat_finish(2 * blk)
-                lat_finish(2 * blk + 1)
+                for k in range(TALL // BLOCK):
+                    lat_finish(blk * (TALL // BLOCK) + k)
             return carry
 
         lax.fori_loop(lo, hi, qd_step, 0)
 
-    mid = half_blk // 2
-    stage2(4)
     stage4(1)
     qd_cut(0, 0, mid)
+    tick_a(5)
+    stage2(4)
+    qd_cut(0, mid, n_tall)
     stage3(3)
-    qd_cut(0, mid, half_blk)
+    stage4(2)
     lat_out = pltpu.make_async_copy(lat_buf, lat_hbm, fin_sem.at[0])
     pe_out = pltpu.make_async_copy(pe_buf, pe_hbm, fin_sem.at[1])
     lat_out.start()
     pe_out.start()
 
+    qd_cut(1, 0, mid)
     tick_a(6)
-    stage4(2)
-    qd_cut(1, 0, mid)
     stage2(5)
-    qd_cut(1, mid, half_blk)
+    qd_cut(1, mid, n_tall)
     stage3(4)
     stage4(3)
     qd_cut(2, 0, mid)
     tick_a(7)
-    qd_cut(2, mid, half_blk)
+    qd_cut(2, mid, n_tall)
     stage2(6)
     stage3(5)
 
@@ -339,13 +353,9 @@
         stage4(unit)
         out_copy(unit - first_out).start()
 
-    plan = [(0, tick_a, 8), (1, stage2, 7), (1, stage3, 6), (3, stage2, 8), (4, stage3, 7), (5, tick_a, 9),
-            (7, stage3, 8), (8, stage4, 5), (8, stage2, 9), (10, tick_a, 10), (12, stage3, 9), (13, stage2, 10),
-            (15, tick_a, 11), (15, finish_out, 9), (16, stage4, 6), (17, stage3, 10), (18, stage2, 11),
-            (20, tick_a, 12), (20, finish_out, 10), (22, stage3, 11), (23, stage2, 12), (24, stage4, 7),
-            (25, tick_a, 13), (25, finish_out, 11), (27, stage3, 12), (28, stage2, 13), (30, finish_out, 12),
-            (32, stage4, 8), (33, stage3, 13), (36, finish_out, 13)]
+    plan = [(0, tick_a, 8), (1, stage2, 7), (2, stage3, 6), (4, tick_a, 9), (5, stage2, 8), (5, stage3, 7), (8, stage4, 5), (9, stage3, 8), (9, stage2, 9), (9, tick_a, 10), (13, stage3, 9), (13, tick_a, 11), (14, stage2, 10), (16, stage4, 6), (17, finish_out, 9), (18, stage3, 10), (18, stage2, 11), (18, tick_a, 12), (22, finish_out, 10), (22, stage3, 11), (22, tick_a, 13), (23, stage2, 12), (24, stage4, 7), (26, finish_out, 11), (27, stage3, 12), (27, stage2, 13), (31, finish_out, 12), (31, stage3, 13), (32, stage4, 8), (35, finish_out, 13)]
     schedule = {}
+    late = [(fn, unit) for at, fn, unit in plan if at >= n_steps]
     for at, fn, unit in plan:
         schedule.setdefault(at, []).append((fn, unit))
     n_pairs = heads_per_group // 2
@@ -441,6 +451,8 @@
         return carry
 
     lax.fori_loop(0, n_steps, attn_step, 0)
+    for fn, unit in late:
+        fn(unit)
 
     for slot in range(2):
         o_copy(0, 0, slot).wait()
@@ -464,18 +476,15 @@
     hpg = n_heads // GROUPS
     half = rope_dim // 2
     cos_s, sin_s = rope_tables(seq_len, rope_dim)
-    pad = jnp.zeros((seq_len, 128 - rope_dim), F32)
-    zero = jnp.zeros((seq_len, half), F32)
-    cos_r = jnp.concatenate([cos_s, cos_s, pad], axis=1)
-    sin_lo = jnp.concatenate([sin_s, zero, pad], axis=1)
-    sin_hi = jnp.concatenate([zero, sin_s, pad], axis=1)
+    pad = np.zeros((seq_len, 128 - rope_dim), np.float32)
+    zero = np.zeros((seq_len, half), np.float32)
+    tab_r = jnp.asarray(np.stack([np.concatenate(parts, axis=1) for parts in (
+        (cos_s, cos_s, pad), (sin_s, zero, pad), (zero, sin_s, pad))]))
     reps = BLOCK // seq_len
-    cos_t = jnp.concatenate([cos_s.T] * reps, axis=1)
-    sin_t = jnp.concatenate([sin_s.T] * reps, axis=1)
+    tab_t = jnp.asarray(np.stack([np.concatenate([t.T] * reps, axis=1) for t in (cos_s, sin_s)]))
     dims = (n_fsdp, seq_len, kv_rank, rope_dim, nope, v_dim, hpg)
     n_pieces = 1 + DQ_CUTS + 2 * GROUPS + OUT_CUTS
     any_spec = pl.BlockSpec(memory_space=pl.ANY)
-    vmem_spec = pl.BlockSpec(memory_space=pltpu.VMEM)
     dma = pltpu.SemaphoreType.DMA
     return pl.pallas_call(
         functools.partial(gather_kernel, dims),
@@ -485,9 +494,11 @@
             jax.ShapeDtypeStruct((n_tok, rope_dim), BF16),
             jax.ShapeDtypeStruct((v_total, d_model), BF16),
         ),
-        in_specs=[any_spec] * 7 + [vmem_spec] * 5,
+        in_specs=[any_spec] * 9,
         out_specs=(any_spec,) * 4,
         scratch_shapes=[
+            pltpu.VMEM(tab_r.shape, F32),
+            pltpu.VMEM(tab_t.shape, F32),
             pltpu.VMEM((n_fsdp,) + gains.shape, F32),
             pltpu.VMEM((dkv_s.shape[0] * n_fsdp, dkv_s.shape[1]), BF16),
             pltpu.VMEM((DQ_CUTS, d_model, q_rank // DQ_CUTS), BF16),
@@ -517,11 +528,12 @@
             dma((n_tok // BLOCK,)),
             dma((2,)),
             dma((2 + OUT_CUTS,)),
+            dma((2,)),
         ],
         compiler_params=pltpu.CompilerParams(
             collective_id=0, has_side_effects=True, vmem_limit_bytes=67043328),
         name='latent_attention',
-    )(x, gains, dq_s, uq_s, dkv_s, ukv_s, out_s, cos_r, sin_lo, sin_hi, cos_t, sin_t)
+    )(x, gains, dq_s, uq_s, dkv_s, ukv_s, out_s, tab_r, tab_t)
 
 
 def solution(mesh):

time: 168 us -> 158 us (0.940)
  Pallas kernels: 125 us -> 117 us
  other arithmetic: 3.09 us -> 1.32 us
    pallas_call x1, Pallas kernels: 125 us -> 117 us  [attention_part(): pl.pallas_call(functools.partial(gather_kernel, dims), out_shape=(jax.Sha...]
where the time goes in v3:
time: 158 us
  Pallas kernels  117 us (74%)
  matrix products  35 us (22%)
  local copies, waits for them, and re-layouts  3.6 us (2%)
    pallas_call x1, Pallas kernels, attention_part(): pl.pallas_call(functools.partial(gather_kernel, dims), out_shape=(jax.Sha...  117 us
    dot_general x1, matrix products, local_block(): proj = jnp.dot(attn_out, w_out_all, preferred_element_type=F32)  35 us
    unnamed x7, local copies, waits for them, and re-layouts  3.6 us

profile of v3, /device:TPU:88, one launch (start us, length us, event | category | flops | bytes accessed | tf_op | source)
XLA Modules:
  0.0 158.1 jit_solution(4888417899192570146)
XLA Ops:
  0.6 0.7 fusion.5
  1.4 0.6 bitcast_convert_fusion.gains_hbm
  2.0 1.8 %copy.14.dkv_hbm = bf16[320,288]{1,0:T(8,128)(2,1)} copy(bf16[320,288]{0,1:T(8,128)(2,1)} %param.16) | data formatting | bytes 368640 | tf_op args[5]
  3.7 117.5 %latent_attention.1 = (bf16[2048,2560]{1,0:T(8,128)(2,1)}, bf16[2048,256]{1,0:T(8,128)(2,1)}, bf16[2048,32]{1,0:T(8,128)(2,1)}, bf16[2560,2560]{1,0:T(8,128)(2,1)}) custom-call(bf16[2048,2560]{1,0:T(8,128)(2,1)} %bitcast.9, f32[8,128]{1,0:T(8,128)} %bitcast_convert_fusion.gains_hbm, bf16[320,768]{1,0:T(8,128)(2,1)} %dq_hbm.1, bf16[96,3840]{1,0:T(8,128)(2,1)} %uq_hbm.1, ...), custom_call_target="tpu_custom_call" | custom-call | tf_op jit(solution)/shard_map/latent_attention/pallas_call | solution.py:489
  121.2 0.0 copy-start.1
  121.2 0.0 copy-start
  121.2 35.0 %add_convert_fusion = bf16[2048,2560]{1,0:T(8,128)(2,1)} fusion(bf16[2048,2560]{1,0:T(8,128)(2,1)} %bitcast.10, bf16[2048,2560]{1,0:T(8,128)(2,1)} %get-tuple-element.7, bf16[2560,2560]{1,0:T(8,128)(2,1)} %get-tuple-element.8), kind=kOutput, calls=%fused_computation | convolution fusion | flops 26859274240 | bytes 44564480 | tf_op jit(solution)/shard_map/dot_general | solution.py:557
  156.3 0.0 copy-done.1
  156.3 0.8 copy.15
  157.1 0.0 copy-done
  157.1 1.0 copy.17
Async XLA Ops:
  121.2 35.1 %copy-start.1 = (bf16[2048,32]{1,0:T(8,128)(2,1)S(1)}, bf16[2048,32]{1,0:T(8,128)(2,1)}, u32[]{:S(2)}) copy-start(bf16[2048,32]{1,0:T(8,128)(2,1)} %get-tuple-element.10) | copy-start | bytes 393220
  121.2 35.9 %copy-start = (bf16[2048,256]{1,0:T(8,128)(2,1)S(1)}, bf16[2048,256]{1,0:T(8,128)(2,1)}, u32[]{:S(2)}) copy-start(bf16[2048,256]{1,0:T(8,128)(2,1)} %get-tuple-element.9) | copy-start | bytes 3145732
